TPU v7x, 512 devices: a whole 4x8x8 slice. The times are simulated.
512 devices in a mesh: cell: 64 (over x, z, core), grp: 8 (over y).
Axes of the slice: x: 4, y: 8, z: 8, core: 2. Of those that a mesh axis runs over, the one named last changes fastest.
Arguments:
- atom_sites: float32 [3, 262144], P(None, ('cell', 'grp')), may hold values from 0 to 64, as said below
- grid_points: float32 [3, 196608], P(None, ('cell', 'grp')), may hold values from 0 to 64, as said below
- dipole_guess: float32 [3, 262144], P(None, ('cell', 'grp')), may hold values from -2 to 2
- fixed_field: float32 [3, 262144], P(None, ('cell', 'grp')), may hold values from -1800 to 1800
- polarisability: float32 [262144], P(('cell', 'grp')), may hold values from 0.0005 to 0.002
- base_charge: float32 [196608], P(('cell', 'grp')), may hold values from -12 to 12
- response: float32 [196608], P(('cell', 'grp')), may hold values from 0.02 to 0.2
- near_blocks: int32 [2048, 8], P(('cell', 'grp')), may hold values from 0 to 95, as said below
- grid_blocks: int32 [2048, 4], P(('cell', 'grp')), may hold values from 0 to 71, as said below
- source_blocks: int32 [1536, 8], P(('cell', 'grp')), may hold values from 0 to 95, as said below
Outputs:
- dipoles: float32 [3, 262144], P(None, ('cell', 'grp'))
- qm_charges: float32 [196608], P(('cell', 'grp'))
Inputs may be any that keep to these rules, and one draw needn't show every extreme that they name: `atom_sites`: atom a has first coordinate in [c, c + 1) with c = a // 4096, the other two in [0, 1). `grid_points`: grid point g has first coordinate in [c, c + 1) with c = g // 3072, the other two in [0, 1). `near_blocks`: each row holds 8 distinct MM window indices, never the block's own index 32 + b % 32. `grid_blocks`: each row holds 4 distinct grid window indices. `source_blocks`: each row holds 8 distinct MM window indices.
All inputs are finite; a program needn't handle non-finite values.
Results may differ from a plain program's by a relative error of at most 0.0003.
Values sent between devices are 32-bit elements; how exact they have to be, the bound alone decides.
No kernel may reach another device: no remote copies, remote signals or barrier semaphores. Data moves between devices by JAX's collectives and lax.ppermute only.
A program may use at most 64 MiB of HBM per device.

v0:
```python
import jax
import jax.numpy as jnp
from jax import lax
from jax.sharding import PartitionSpec as P

BLOCK = 128
ITERS = 3


soften_sq = 0.04


def laid_out(pieces, dim):
    pieces = jnp.moveaxis(pieces, 0, dim)
    lengths = pieces.shape
    return pieces.reshape(*lengths[:dim], lengths[dim] * lengths[dim + 1], *lengths[dim + 2 :])


def copy_for_each(x, axis):
    copies = jnp.broadcast_to(x, (lax.axis_size(axis), *x.shape))
    return lax.all_to_all(copies, axis, split_axis=0, concat_axis=0, tiled=True)


def gather_directly(x, axis, dim):
    return laid_out(copy_for_each(x, axis), dim)


def with_halo(x, sides, width):
    for axis, dim in sides:
        peers, length = (lax.axis_size(axis), x.shape[dim])
        up = [(i, (i + 1) % peers) for i in range(peers - 1)]
        down = [(j, i) for i, j in up]
        last = lax.slice_in_dim(x, length - width, length, axis=dim)
        initial = lax.slice_in_dim(x, 0, width, axis=dim)
        before = lax.ppermute(last, axis, up)
        after = lax.ppermute(initial, axis, down)
        x = jnp.concatenate([before, x, after], axis=dim)
    return x


def taken_together(x, axis):
    everything = copy_for_each(x, axis)
    return jnp.sum(everything, axis=0)


def pair_geometry(targets, sources):
    delta_x = targets[0][:, None] - sources[0][None, :]
    delta_y = targets[1][:, None] - sources[1][None, :]
    delta_z = targets[2][:, None] - sources[2][None, :]
    inverse = 1.0 / jnp.sqrt(delta_x * delta_x + delta_y * delta_y + delta_z * delta_z + soften_sq)
    inv_cube = inverse * inverse * inverse
    return (delta_x, delta_y, delta_z, inv_cube, inv_cube * inverse * inverse)


def dipole_field(targets, sources, moments, keep_mask):
    delta_x, delta_y, delta_z, inv_cube, inv_fifth = pair_geometry(targets, sources)
    projected = (
        moments[0][None, :] * delta_x
        + moments[1][None, :] * delta_y
        + moments[2][None, :] * delta_z
    )
    radial = 3.0 * projected * inv_fifth * keep_mask
    direct = inv_cube * keep_mask
    return jnp.stack(
        [
            jnp.sum(radial * delta_x - moments[0][None, :] * direct, axis=1),
            jnp.sum(radial * delta_y - moments[1][None, :] * direct, axis=1),
            jnp.sum(radial * delta_z - moments[2][None, :] * direct, axis=1),
        ]
    )


def charge_field(targets, sources, charges):
    delta_x, delta_y, delta_z, inv_cube, inv_fifth = pair_geometry(targets, sources)
    weight = charges[None, :] * inv_cube
    return jnp.stack(
        [
            jnp.sum(weight * delta_x, axis=1),
            jnp.sum(weight * delta_y, axis=1),
            jnp.sum(weight * delta_z, axis=1),
        ]
    )


def dipole_potential(targets, sources, moments):
    delta_x, delta_y, delta_z, inv_cube, inv_fifth = pair_geometry(targets, sources)
    projected = (
        moments[0][None, :] * delta_x
        + moments[1][None, :] * delta_y
        + moments[2][None, :] * delta_z
    )
    return jnp.sum(projected * inv_cube, axis=1)


def far_geometry(targets, cell_here, cell_count):
    centres = jnp.arange(cell_count, dtype=jnp.int32).astype(jnp.float32) + 0.5
    delta_x = targets[0][None, :] - centres[:, None]
    delta_y = targets[1][None, :] - 0.5
    delta_z = targets[2][None, :] - 0.5
    far_mask = (jnp.abs(jnp.arange(cell_count, dtype=jnp.int32) - cell_here) >= 2).astype(
        jnp.float32
    )[:, None]
    inverse = 1.0 / jnp.sqrt(delta_x * delta_x + delta_y * delta_y + delta_z * delta_z + soften_sq)
    inv_cube = inverse * inverse * inverse * far_mask
    return (delta_x, delta_y, delta_z, inv_cube, inv_cube * inverse * inverse)


def far_field(targets, cell_here, moments, charges):
    delta_x, delta_y, delta_z, inv_cube, inv_fifth = far_geometry(
        targets, cell_here, charges.shape[0]
    )
    projected = moments[:, 0:1] * delta_x + moments[:, 1:2] * delta_y + moments[:, 2:3] * delta_z
    radial = 3.0 * projected * inv_fifth
    coulomb = charges[:, None] * inv_cube
    return jnp.stack(
        [
            jnp.sum(radial * delta_x - moments[:, 0:1] * inv_cube + coulomb * delta_x, axis=0),
            jnp.sum(radial * delta_y - moments[:, 1:2] * inv_cube + coulomb * delta_y, axis=0),
            jnp.sum(radial * delta_z - moments[:, 2:3] * inv_cube + coulomb * delta_z, axis=0),
        ]
    )


def far_potential(targets, cell_here, moments):
    delta_x, delta_y, delta_z, inv_cube, inv_fifth = far_geometry(
        targets, cell_here, moments.shape[0]
    )
    projected = moments[:, 0:1] * delta_x + moments[:, 1:2] * delta_y + moments[:, 2:3] * delta_z
    return jnp.sum(projected * inv_cube, axis=0)


def listed_tiles(tile_set, index_lists):
    taken = jnp.take(tile_set, index_lists, axis=1)
    count, listed = index_lists.shape
    return jnp.transpose(taken, (1, 0, 2, 3)).reshape(count, 3, listed * tile_set.shape[2])


def spread(payload):
    lifted = payload[:, None, None, :]
    members = gather_directly(lifted, "grp", 2)
    return with_halo(members, (("cell", 1),), 1)


def body(
    atom_sites,
    grid_points,
    dipole_guess,
    fixed_field,
    polarisability,
    base_charge,
    response,
    near_blocks,
    grid_blocks,
    source_blocks,
):
    groups = lax.axis_size("grp")
    cell_here = lax.axis_index("cell")
    grp_here = lax.axis_index("grp")
    local_blocks = near_blocks.shape[0]
    local_gblocks = source_blocks.shape[0]
    atom_count = atom_sites.shape[1]
    grid_count = grid_points.shape[1]
    cell_blocks = local_blocks * groups
    cell_gblocks = local_gblocks * groups
    statics = spread(jnp.concatenate([atom_sites, grid_points], axis=1))
    site_tiles = statics[:, :, :, :atom_count].reshape(3, 3 * cell_blocks, BLOCK)
    point_tiles = statics[:, :, :, atom_count:].reshape(3, 3 * cell_gblocks, BLOCK)
    atom_targets = jnp.transpose(atom_sites.reshape(3, local_blocks, BLOCK), (1, 0, 2))
    grid_targets = jnp.transpose(grid_points.reshape(3, local_gblocks, BLOCK), (1, 0, 2))
    own_slots = cell_blocks + grp_here * local_blocks + jnp.arange(local_blocks, dtype=jnp.int32)
    atom_lists = jnp.concatenate([own_slots[:, None], near_blocks], axis=1)
    near_sites = listed_tiles(site_tiles, atom_lists)
    grid_sites = listed_tiles(point_tiles, grid_blocks)
    source_sites = listed_tiles(site_tiles, source_blocks)
    keep_mask = jnp.concatenate(
        [
            1.0 - jnp.eye(BLOCK, dtype=jnp.float32),
            jnp.ones((BLOCK, near_blocks.shape[1] * BLOCK), jnp.float32),
        ],
        axis=1,
    )
    centre = jnp.stack(
        [
            cell_here.astype(jnp.float32) + 0.5,
            jnp.array(0.5, jnp.float32),
            jnp.array(0.5, jnp.float32),
        ]
    )
    offsets = grid_points - centre[:, None]
    dipoles = dipole_guess
    charges = base_charge
    for iteration in range(ITERS):
        shared = spread(jnp.concatenate([dipoles, charges.reshape(3, grid_count // 3)], axis=1))
        dipole_tiles = shared[:, :, :, :atom_count].reshape(3, 3 * cell_blocks, BLOCK)
        charge_tiles = jnp.transpose(shared[:, :, :, atom_count:], (1, 2, 0, 3)).reshape(
            3 * cell_gblocks, BLOCK
        )
        local_sums = jnp.concatenate(
            [
                jnp.sum(dipoles, axis=1),
                jnp.sum(charges)[None],
                jnp.sum(charges[None, :] * offsets, axis=1),
            ]
        )
        cell_sums = taken_together(local_sums, "grp")
        moment_table = gather_directly(cell_sums[None, :], "cell", 0)
        dipole_sums = moment_table[:, 0:3]
        charge_sums = moment_table[:, 3]
        moments = dipole_sums + moment_table[:, 4:7]
        near_dipoles = listed_tiles(dipole_tiles, atom_lists)
        source_dipoles = listed_tiles(dipole_tiles, source_blocks)
        grid_charges = jnp.take(charge_tiles, grid_blocks, axis=0).reshape(local_blocks, -1)

        def one_atom_block(block_args):
            targets, sources, source_moments, points, point_charges = block_args
            accumulated = dipole_field(targets, sources, source_moments, keep_mask)
            accumulated = accumulated + charge_field(targets, points, point_charges)
            return accumulated + far_field(targets, cell_here, moments, charge_sums)

        def one_grid_block(block_args):
            targets, sources, source_moments = block_args
            return dipole_potential(targets, sources, source_moments) + far_potential(
                targets, cell_here, dipole_sums
            )

        induced_field = lax.map(
            one_atom_block, (atom_targets, near_sites, near_dipoles, grid_sites, grid_charges)
        )
        induced_field = jnp.transpose(induced_field, (1, 0, 2)).reshape(3, atom_count)
        potential = lax.map(one_grid_block, (grid_targets, source_sites, source_dipoles)).reshape(
            grid_count
        )
        dipoles = polarisability[None, :] * (fixed_field + induced_field)
        charges = base_charge - response * potential
    return (dipoles, charges)


def solution(mesh):
    return jax.shard_map(
        body,
        mesh=mesh,
        in_specs=(
            P(None, ("cell", "grp")),
            P(None, ("cell", "grp")),
            P(None, ("cell", "grp")),
            P(None, ("cell", "grp")),
            P(("cell", "grp")),
            P(("cell", "grp")),
            P(("cell", "grp")),
            P(("cell", "grp"), None),
            P(("cell", "grp"), None),
            P(("cell", "grp"), None),
        ),
        out_specs=(P(None, ("cell", "grp")), P(("cell", "grp"))),
        check_vma=False,
    )
```

profile of v0, /device:TPU:1, one launch (start us, length us, event | category | flops | bytes accessed | tf_op | source)
XLA Modules:
  0.0 200.5 jit_solution(17839278385963394076)
XLA Ops:
  0.7 0.7 copy-done.2
  2.2 0.7 pad_maximum_fusion.9
  3.6 7.8 %all-to-all-start.2 = ((f32[8,1,7]{2,1,0:T(1,128)}), f32[8,1,7]{2,1,0:T(1,128)S(1)}, u32[]{:S(2)}, u32[]{:S(2)}) async-start(f32[8,1,7]{2,1,0:T(1,128)} %broadcast_in_dim.122), calls=%async_computation.2 | async-start | bytes 8192 | tf_op jit(solution)/shard_map/all_to_all | solution.py:21
  11.4 0.7 copy-done.8
  12.2 0.7 copy-done.1
  12.9 0.7 copy-done.9
  13.8 4.0 %all-to-all-done.2 = f32[8,1,7]{2,1,0:T(1,128)S(1)} async-done(((f32[8,1,7]{2,1,0:T(1,128)}), f32[8,1,7]{2,1,0:T(1,128)S(1)}, u32[]{:S(2)}, u32[]{:S(2)}) %all-to-all-start.2) | async-done | bytes 256 | tf_op jit(solution)/shard_map/all_to_all | solution.py:21
  17.8 0.7 broadcast_in_dim.116
  18.5 3.3 %all-to-all-start = ((f32[8,3,1,1,640]{4,3,2,1,0:T(1,128)}), f32[8,3,1,1,640]{4,3,2,1,0:T(1,128)S(1)}, u32[]{:S(2)}, u32[]{:S(2)}) async-start(f32[8,3,1,1,640]{4,3,2,1,0:T(1,128)} %broadcast_in_dim.116), calls=%async_computation | async-start | bytes 122880 | tf_op jit(solution)/shard_map/all_to_all | solution.py:21
  21.9 7.1 %all-to-all-done = f32[8,3,1,1,640]{4,3,2,1,0:T(1,128)S(1)} async-done(((f32[8,3,1,1,640]{4,3,2,1,0:T(1,128)}), f32[8,3,1,1,640]{4,3,2,1,0:T(1,128)S(1)}, u32[]{:S(2)}, u32[]{:S(2)}) %all-to-all-start) | async-done | bytes 61472 | tf_op jit(solution)/shard_map/all_to_all | solution.py:21
  28.9 0.6 broadcast_in_dim.123
  29.6 16.6 %all-to-all-start.3 = ((f32[64,1,7]{2,1,0:T(1,128)}), f32[64,1,7]{2,1,0:T(1,128)S(1)}, u32[]{:S(2)}, u32[]{:S(2)}) async-start(f32[64,1,7]{2,1,0:T(1,128)} %broadcast_in_dim.123), calls=%async_computation.3 | async-start | bytes 65536 | tf_op jit(solution)/shard_map/all_to_all | solution.py:21
  46.2 2.4 %collective-permute-start.1 = (f32[3,1,8,640]{3,2,0,1:T(8,128)S(1)}, f32[3,1,8,640]{3,2,0,1:T(8,128)S(1)}, u32[]{:S(2)}, u32[]{:S(2)}) collective-permute-start(f32[3,1,8,640]{3,2,0,1:T(8,128)S(1)} %bitcast.555), channel_id=1, source_target_pairs={{8,0},{16,8},{24,16},{32,24},{40,32},{48,40},{56,48},{64,56},{72,6... | collective-permute-start | bytes 184328 | tf_op jit(solution)/shard_map/ppermute | solution.py:36
  48.6 3.2 %collective-permute-start = (f32[3,1,8,640]{3,2,0,1:T(8,128)S(1)}, f32[3,1,8,640]{3,2,0,1:T(8,128)S(1)}, u32[]{:S(2)}, u32[]{:S(2)}) collective-permute-start(f32[3,1,8,640]{3,2,0,1:T(8,128)S(1)} %bitcast.556), channel_id=1, source_target_pairs={{0,8},{8,16},{16,24},{24,32},{32,40},{40,48},{48,56},{56,64},{64,7... | collective-permute-start | bytes 184328 | tf_op jit(solution)/shard_map/ppermute | solution.py:35
  51.8 3.7 %all-to-all-done.3 = f32[64,1,7]{2,1,0:T(1,128)S(1)} async-done(((f32[64,1,7]{2,1,0:T(1,128)}), f32[64,1,7]{2,1,0:T(1,128)S(1)}, u32[]{:S(2)}, u32[]{:S(2)}) %all-to-all-start.3) | async-done | bytes 1824 | tf_op jit(solution)/shard_map/all_to_all | solution.py:21
  55.5 0.7 broadcast_in_dim.117
  56.1 3.4 %all-to-all-start.1 = ((f32[8,3,1,1,896]{4,3,2,1,0:T(1,128)}), f32[8,3,1,1,896]{4,3,2,1,0:T(1,128)S(1)}, u32[]{:S(2)}, u32[]{:S(2)}) async-start(f32[8,3,1,1,896]{4,3,2,1,0:T(1,128)} %broadcast_in_dim.117), calls=%async_computation.1 | async-start | bytes 172032 | tf_op jit(solution)/shard_map/all_to_all | solution.py:21
  59.9 7.0 %all-to-all-done.1 = f32[8,3,1,1,896]{4,3,2,1,0:T(1,128)S(1)} async-done(((f32[8,3,1,1,896]{4,3,2,1,0:T(1,128)}), f32[8,3,1,1,896]{4,3,2,1,0:T(1,128)S(1)}, u32[]{:S(2)}, u32[]{:S(2)}) %all-to-all-start.1) | async-done | bytes 86048 | tf_op jit(solution)/shard_map/all_to_all | solution.py:21
  66.9 3.7 %collective-permute-start.3 = (f32[3,1,8,896]{3,2,0,1:T(8,128)S(1)}, f32[3,1,8,896]{3,2,0,1:T(8,128)S(1)}, u32[]{:S(2)}, u32[]{:S(2)}) collective-permute-start(f32[3,1,8,896]{3,2,0,1:T(8,128)S(1)} %bitcast.551), channel_id=1, source_target_pairs={{8,0},{16,8},{24,16},{32,24},{40,32},{48,40},{56,48},{64,56},{72,6... | collective-permute-start | bytes 258056 | tf_op jit(solution)/shard_map/ppermute | solution.py:36
  70.6 2.2 %collective-permute-start.2 = (f32[3,1,8,896]{3,2,0,1:T(8,128)S(1)}, f32[3,1,8,896]{3,2,0,1:T(8,128)S(1)}, u32[]{:S(2)}, u32[]{:S(2)}) collective-permute-start(f32[3,1,8,896]{3,2,0,1:T(8,128)S(1)} %bitcast.552), channel_id=1, source_target_pairs={{0,8},{8,16},{16,24},{24,32},{32,40},{40,48},{48,56},{56,64},{64,7... | collective-permute-start | bytes 258056 | tf_op jit(solution)/shard_map/ppermute | solution.py:35
  74.3 0.6 gather_fusion.1
  75.7 0.6 gather_fusion.2
  77.3 2.5 %while.79 = (s32[]{:T(128)}, f32[3,128]{1,0:T(4,128)S(1)}, f32[3,3,1024]{2,0,1:T(4,128)S(1)}, f32[3,3,128]{2,1,0:T(4,128)S(1)}, f32[3,3,1024]{2,1,0:T(4,128)S(1)...) while((s32[]{:T(128)}, f32[3,128]{1,0:T(4,128)S(1)}, ...), condition=%wide.region_18.22_spmd, body=%wide.region_15.21_spmd.sunk | while | flops 2482948 | bytes 94129 | solution.py:230
  80.8 6.5 %while.78 = (s32[]{:T(128)}, f32[4,3,128]{2,1,0:T(4,128)S(1)}, f32[4,3,1152]{2,1,0:T(4,128)S(1)}, f32[4,3,128]{2,1,0:T(4,128)S(1)}, f32[4,3,1152]{2,1,0:T(4,128)...) while((s32[]{:T(128)}, f32[4,3,128]{2,1,0:T(4,128)S(1)}, ...), condition=%wide.region_14.17_spmd, body=%wide.region_4.16_spmd.sunk | while | flops 6490884 | bytes 727253 | solution.py:226
  81.5 0.9 fusion.208
  83.1 0.9 fusion.208
  84.7 0.9 fusion.208
  86.4 0.9 fusion.208
  87.4 0.7 pad_maximum_fusion.10
  88.7 3.3 %all-to-all-start.5 = ((f32[8,1,7]{2,1,0:T(1,128)}), f32[8,1,7]{2,1,0:T(1,128)S(1)}, u32[]{:S(2)}, u32[]{:S(2)}) async-start(f32[8,1,7]{2,1,0:T(1,128)} %broadcast_in_dim.126), calls=%async_computation.5 | async-start | bytes 8192 | tf_op jit(solution)/shard_map/all_to_all | solution.py:21
  92.1 6.4 %all-to-all-done.5 = f32[8,1,7]{2,1,0:T(1,128)S(1)} async-done(((f32[8,1,7]{2,1,0:T(1,128)}), f32[8,1,7]{2,1,0:T(1,128)S(1)}, u32[]{:S(2)}, u32[]{:S(2)}) %all-to-all-start.5) | async-done | bytes 256 | tf_op jit(solution)/shard_map/all_to_all | solution.py:21
  98.5 0.7 broadcast_in_dim.124
  99.1 3.3 %all-to-all-start.4 = ((f32[8,3,1,1,640]{4,3,2,1,0:T(1,128)}), f32[8,3,1,1,640]{4,3,2,1,0:T(1,128)S(1)}, u32[]{:S(2)}, u32[]{:S(2)}) async-start(f32[8,3,1,1,640]{4,3,2,1,0:T(1,128)} %broadcast_in_dim.124), calls=%async_computation.4 | async-start | bytes 122880 | tf_op jit(solution)/shard_map/all_to_all | solution.py:21
  102.5 7.1 %all-to-all-done.4 = f32[8,3,1,1,640]{4,3,2,1,0:T(1,128)S(1)} async-done(((f32[8,3,1,1,640]{4,3,2,1,0:T(1,128)}), f32[8,3,1,1,640]{4,3,2,1,0:T(1,128)S(1)}, u32[]{:S(2)}, u32[]{:S(2)}) %all-to-all-start.4) | async-done | bytes 61472 | tf_op jit(solution)/shard_map/all_to_all | solution.py:21
  109.6 0.6 broadcast_in_dim.127
  110.2 11.4 %all-to-all-start.6 = ((f32[64,1,7]{2,1,0:T(1,128)}), f32[64,1,7]{2,1,0:T(1,128)S(1)}, u32[]{:S(2)}, u32[]{:S(2)}) async-start(f32[64,1,7]{2,1,0:T(1,128)} %broadcast_in_dim.127), calls=%async_computation.6 | async-start | bytes 65536 | tf_op jit(solution)/shard_map/all_to_all | solution.py:21
  121.6 2.4 %collective-permute-start.5 = (f32[3,1,8,640]{3,2,0,1:T(8,128)S(1)}, f32[3,1,8,640]{3,2,0,1:T(8,128)S(1)}, u32[]{:S(2)}, u32[]{:S(2)}) collective-permute-start(f32[3,1,8,640]{3,2,0,1:T(8,128)S(1)} %bitcast.563), channel_id=1, source_target_pairs={{8,0},{16,8},{24,16},{32,24},{40,32},{48,40},{56,48},{64,56},{72,6... | collective-permute-start | bytes 184328 | tf_op jit(solution)/shard_map/ppermute | solution.py:36
  124.0 3.2 %collective-permute-start.4 = (f32[3,1,8,640]{3,2,0,1:T(8,128)S(1)}, f32[3,1,8,640]{3,2,0,1:T(8,128)S(1)}, u32[]{:S(2)}, u32[]{:S(2)}) collective-permute-start(f32[3,1,8,640]{3,2,0,1:T(8,128)S(1)} %bitcast.564), channel_id=1, source_target_pairs={{0,8},{8,16},{16,24},{24,32},{32,40},{40,48},{48,56},{56,64},{64,7... | collective-permute-start | bytes 184328 | tf_op jit(solution)/shard_map/ppermute | solution.py:35
  127.2 3.7 %all-to-all-done.6 = f32[64,1,7]{2,1,0:T(1,128)S(1)} async-done(((f32[64,1,7]{2,1,0:T(1,128)}), f32[64,1,7]{2,1,0:T(1,128)S(1)}, u32[]{:S(2)}, u32[]{:S(2)}) %all-to-all-start.6) | async-done | bytes 1824 | tf_op jit(solution)/shard_map/all_to_all | solution.py:21
  132.1 0.6 gather_fusion.6
  133.6 6.5 %while.80 = (s32[]{:T(128)}, f32[4,3,128]{2,1,0:T(4,128)S(1)}, f32[4,3,1152]{2,1,0:T(4,128)S(1)}, f32[4,3,128]{2,1,0:T(4,128)S(1)}, f32[4,3,1152]{2,1,0:T(4,128)...) while((s32[]{:T(128)}, f32[4,3,128]{2,1,0:T(4,128)S(1)}, ...), condition=%wide.region_33.37_spmd, body=%wide.region_23.36_spmd.sunk | while | flops 6490884 | bytes 727253 | solution.py:226
  134.3 0.9 fusion.213
  135.9 0.9 fusion.213
  137.6 0.9 fusion.213
  139.2 0.9 fusion.213
  140.3 2.5 %while.81 = (s32[]{:T(128)}, f32[3,128]{1,0:T(4,128)S(1)}, f32[3,3,1024]{2,0,1:T(4,128)S(1)}, f32[3,3,128]{2,1,0:T(4,128)S(1)}, f32[3,3,1024]{2,1,0:T(4,128)S(1)...) while((s32[]{:T(128)}, f32[3,128]{1,0:T(4,128)S(1)}, ...), condition=%wide.region_37.41_spmd, body=%wide.region_34.40_spmd.sunk | while | flops 2482948 | bytes 94129 | solution.py:230
  143.6 0.7 pad_maximum_fusion.11
  144.9 3.3 %all-to-all-start.8 = ((f32[8,1,7]{2,1,0:T(1,128)}), f32[8,1,7]{2,1,0:T(1,128)S(1)}, u32[]{:S(2)}, u32[]{:S(2)}) async-start(f32[8,1,7]{2,1,0:T(1,128)} %broadcast_in_dim.130), calls=%async_computation.8 | async-start | bytes 8192 | tf_op jit(solution)/shard_map/all_to_all | solution.py:21
  148.2 6.4 %all-to-all-done.8 = f32[8,1,7]{2,1,0:T(1,128)S(1)} async-done(((f32[8,1,7]{2,1,0:T(1,128)}), f32[8,1,7]{2,1,0:T(1,128)S(1)}, u32[]{:S(2)}, u32[]{:S(2)}) %all-to-all-start.8) | async-done | bytes 256 | tf_op jit(solution)/shard_map/all_to_all | solution.py:21
  154.6 0.7 broadcast_in_dim.128
  155.3 3.3 %all-to-all-start.7 = ((f32[8,3,1,1,640]{4,3,2,1,0:T(1,128)}), f32[8,3,1,1,640]{4,3,2,1,0:T(1,128)S(1)}, u32[]{:S(2)}, u32[]{:S(2)}) async-start(f32[8,3,1,1,640]{4,3,2,1,0:T(1,128)} %broadcast_in_dim.128), calls=%async_computation.7 | async-start | bytes 122880 | tf_op jit(solution)/shard_map/all_to_all | solution.py:21
  158.7 7.2 %all-to-all-done.7 = f32[8,3,1,1,640]{4,3,2,1,0:T(1,128)S(1)} async-done(((f32[8,3,1,1,640]{4,3,2,1,0:T(1,128)}), f32[8,3,1,1,640]{4,3,2,1,0:T(1,128)S(1)}, u32[]{:S(2)}, u32[]{:S(2)}) %all-to-all-start.7) | async-done | bytes 61472 | tf_op jit(solution)/shard_map/all_to_all | solution.py:21
  165.8 0.6 broadcast_in_dim.131
  166.4 11.7 %all-to-all-start.9 = ((f32[64,1,7]{2,1,0:T(1,128)}), f32[64,1,7]{2,1,0:T(1,128)S(1)}, u32[]{:S(2)}, u32[]{:S(2)}) async-start(f32[64,1,7]{2,1,0:T(1,128)} %broadcast_in_dim.131), calls=%async_computation.9 | async-start | bytes 65536 | tf_op jit(solution)/shard_map/all_to_all | solution.py:21
  178.2 2.4 %collective-permute-start.7 = (f32[3,1,8,640]{3,2,0,1:T(8,128)S(1)}, f32[3,1,8,640]{3,2,0,1:T(8,128)S(1)}, u32[]{:S(2)}, u32[]{:S(2)}) collective-permute-start(f32[3,1,8,640]{3,2,0,1:T(8,128)S(1)} %bitcast.559), channel_id=1, source_target_pairs={{8,0},{16,8},{24,16},{32,24},{40,32},{48,40},{56,48},{64,56},{72,6... | collective-permute-start | bytes 184328 | tf_op jit(solution)/shard_map/ppermute | solution.py:36
  180.6 3.4 %collective-permute-start.6 = (f32[3,1,8,640]{3,2,0,1:T(8,128)S(1)}, f32[3,1,8,640]{3,2,0,1:T(8,128)S(1)}, u32[]{:S(2)}, u32[]{:S(2)}) collective-permute-start(f32[3,1,8,640]{3,2,0,1:T(8,128)S(1)} %bitcast.560), channel_id=1, source_target_pairs={{0,8},{8,16},{16,24},{24,32},{32,40},{40,48},{48,56},{56,64},{64,7... | collective-permute-start | bytes 184328 | tf_op jit(solution)/shard_map/ppermute | solution.py:35
  184.0 3.5 %all-to-all-done.9 = f32[64,1,7]{2,1,0:T(1,128)S(1)} async-done(((f32[64,1,7]{2,1,0:T(1,128)}), f32[64,1,7]{2,1,0:T(1,128)S(1)}, u32[]{:S(2)}, u32[]{:S(2)}) %all-to-all-start.9) | async-done | bytes 1824 | tf_op jit(solution)/shard_map/all_to_all | solution.py:21
  188.7 0.6 gather_fusion.9
  190.2 6.5 %while.82 = (s32[]{:T(128)}, f32[4,3,128]{2,1,0:T(4,128)S(1)}, f32[4,3,1152]{2,1,0:T(4,128)S(1)}, f32[4,3,128]{2,1,0:T(4,128)S(1)}, f32[4,3,1152]{2,1,0:T(4,128)...) while((s32[]{:T(128)}, f32[4,3,128]{2,1,0:T(4,128)S(1)}, ...), condition=%wide.region_52.56_spmd, body=%wide.region_42.55_spmd.sunk | while | flops 6490884 | bytes 727253 | solution.py:226
  190.9 0.9 fusion.218
  192.6 0.9 fusion.218
  194.2 0.9 fusion.218
  195.8 0.9 fusion.218
  197.4 2.5 %while.83 = (s32[]{:T(128)}, f32[3,128]{1,0:T(4,128)S(1)}, f32[3,3,1024]{2,0,1:T(4,128)S(1)}, f32[3,3,128]{2,1,0:T(4,128)S(1)}, f32[3,3,1024]{2,1,0:T(4,128)S(1)...) while((s32[]{:T(128)}, f32[3,128]{1,0:T(4,128)S(1)}, ...), condition=%wide.region_56.60_spmd, body=%wide.region_53.59_spmd.sunk | while | flops 2482948 | bytes 94129 | solution.py:230
  (399 shorter events, 28.6 us)
Async XLA Ops:
  0.6 1.3 copy-start.4
  0.6 0.7 copy-start.2
  1.3 0.7 copy-start
  3.6 7.8 %copy-start.7 = (s32[4,4]{1,0:T(4,128)S(1)}, s32[4,4]{1,0:T(4,128)}, u32[]{:S(2)}) copy-start(s32[4,4]{1,0:T(4,128)} %param.36) | copy-start | bytes 196
  3.6 14.3 %all-to-all-start.2 = ((f32[8,1,7]{2,1,0:T(1,128)}), f32[8,1,7]{2,1,0:T(1,128)S(1)}, u32[]{:S(2)}, u32[]{:S(2)}) async-start(f32[8,1,7]{2,1,0:T(1,128)} %broadcast_in_dim.122), calls=%async_computation.2 | async-start | bytes 8192 | tf_op jit(solution)/shard_map/all_to_all | solution.py:21
  11.4 0.7 copy-start.8
  12.2 0.7 copy-start.1
  12.9 0.7 copy-start.9
  18.5 10.5 %all-to-all-start = ((f32[8,3,1,1,640]{4,3,2,1,0:T(1,128)}), f32[8,3,1,1,640]{4,3,2,1,0:T(1,128)S(1)}, u32[]{:S(2)}, u32[]{:S(2)}) async-start(f32[8,3,1,1,640]{4,3,2,1,0:T(1,128)} %broadcast_in_dim.116), calls=%async_computation | async-start | bytes 122880 | tf_op jit(solution)/shard_map/all_to_all | solution.py:21
  29.6 25.9 %all-to-all-start.3 = ((f32[64,1,7]{2,1,0:T(1,128)}), f32[64,1,7]{2,1,0:T(1,128)S(1)}, u32[]{:S(2)}, u32[]{:S(2)}) async-start(f32[64,1,7]{2,1,0:T(1,128)} %broadcast_in_dim.123), calls=%async_computation.3 | async-start | bytes 65536 | tf_op jit(solution)/shard_map/all_to_all | solution.py:21
  46.2 26.5 %collective-permute-start.1 = (f32[3,1,8,640]{3,2,0,1:T(8,128)S(1)}, f32[3,1,8,640]{3,2,0,1:T(8,128)S(1)}, u32[]{:S(2)}, u32[]{:S(2)}) collective-permute-start(f32[3,1,8,640]{3,2,0,1:T(8,128)S(1)} %bitcast.555), channel_id=1, source_target_pairs={{8,0},{16,8},{24,16},{32,24},{40,32},{48,40},{56,48},{64,56},{72,6... | collective-permute-start | bytes 184328 | tf_op jit(solution)/shard_map/ppermute | solution.py:36
  48.6 24.2 %collective-permute-start = (f32[3,1,8,640]{3,2,0,1:T(8,128)S(1)}, f32[3,1,8,640]{3,2,0,1:T(8,128)S(1)}, u32[]{:S(2)}, u32[]{:S(2)}) collective-permute-start(f32[3,1,8,640]{3,2,0,1:T(8,128)S(1)} %bitcast.556), channel_id=1, source_target_pairs={{0,8},{8,16},{16,24},{24,32},{32,40},{40,48},{48,56},{56,64},{64,7... | collective-permute-start | bytes 184328 | tf_op jit(solution)/shard_map/ppermute | solution.py:35
  56.1 10.7 %all-to-all-start.1 = ((f32[8,3,1,1,896]{4,3,2,1,0:T(1,128)}), f32[8,3,1,1,896]{4,3,2,1,0:T(1,128)S(1)}, u32[]{:S(2)}, u32[]{:S(2)}) async-start(f32[8,3,1,1,896]{4,3,2,1,0:T(1,128)} %broadcast_in_dim.117), calls=%async_computation.1 | async-start | bytes 172032 | tf_op jit(solution)/shard_map/all_to_all | solution.py:21
  66.9 8.0 %collective-permute-start.3 = (f32[3,1,8,896]{3,2,0,1:T(8,128)S(1)}, f32[3,1,8,896]{3,2,0,1:T(8,128)S(1)}, u32[]{:S(2)}, u32[]{:S(2)}) collective-permute-start(f32[3,1,8,896]{3,2,0,1:T(8,128)S(1)} %bitcast.551), channel_id=1, source_target_pairs={{8,0},{16,8},{24,16},{32,24},{40,32},{48,40},{56,48},{64,56},{72,6... | collective-permute-start | bytes 258056 | tf_op jit(solution)/shard_map/ppermute | solution.py:36
  70.6 4.3 %collective-permute-start.2 = (f32[3,1,8,896]{3,2,0,1:T(8,128)S(1)}, f32[3,1,8,896]{3,2,0,1:T(8,128)S(1)}, u32[]{:S(2)}, u32[]{:S(2)}) collective-permute-start(f32[3,1,8,896]{3,2,0,1:T(8,128)S(1)} %bitcast.552), channel_id=1, source_target_pairs={{0,8},{8,16},{16,24},{24,32},{32,40},{40,48},{48,56},{56,64},{64,7... | collective-permute-start | bytes 258056 | tf_op jit(solution)/shard_map/ppermute | solution.py:35
  77.3 2.6 %copy-start.5 = (f32[384]{0:T(512)S(1)}, f32[384]{0:T(512)}, u32[]{:S(2)}) copy-start(f32[384]{0:T(512)} %param.34) | copy-start | bytes 4612
  80.8 6.5 %copy-start.3 = (f32[3,512]{1,0:T(4,128)S(1)}, f32[3,512]{1,0:T(4,128)}, u32[]{:S(2)}) copy-start(f32[3,512]{1,0:T(4,128)} %param.31) | copy-start | bytes 18436
  80.8 6.5 %copy-start.6 = (f32[512]{0:T(512)S(1)}, f32[512]{0:T(512)}, u32[]{:S(2)}) copy-start(f32[512]{0:T(512)} %param.32) | copy-start | bytes 6148
  88.7 9.7 %all-to-all-start.5 = ((f32[8,1,7]{2,1,0:T(1,128)}), f32[8,1,7]{2,1,0:T(1,128)S(1)}, u32[]{:S(2)}, u32[]{:S(2)}) async-start(f32[8,1,7]{2,1,0:T(1,128)} %broadcast_in_dim.126), calls=%async_computation.5 | async-start | bytes 8192 | tf_op jit(solution)/shard_map/all_to_all | solution.py:21
  99.1 10.5 %all-to-all-start.4 = ((f32[8,3,1,1,640]{4,3,2,1,0:T(1,128)}), f32[8,3,1,1,640]{4,3,2,1,0:T(1,128)S(1)}, u32[]{:S(2)}, u32[]{:S(2)}) async-start(f32[8,3,1,1,640]{4,3,2,1,0:T(1,128)} %broadcast_in_dim.124), calls=%async_computation.4 | async-start | bytes 122880 | tf_op jit(solution)/shard_map/all_to_all | solution.py:21
  110.2 20.7 %all-to-all-start.6 = ((f32[64,1,7]{2,1,0:T(1,128)}), f32[64,1,7]{2,1,0:T(1,128)S(1)}, u32[]{:S(2)}, u32[]{:S(2)}) async-start(f32[64,1,7]{2,1,0:T(1,128)} %broadcast_in_dim.127), calls=%async_computation.6 | async-start | bytes 65536 | tf_op jit(solution)/shard_map/all_to_all | solution.py:21
  121.6 9.7 %collective-permute-start.5 = (f32[3,1,8,640]{3,2,0,1:T(8,128)S(1)}, f32[3,1,8,640]{3,2,0,1:T(8,128)S(1)}, u32[]{:S(2)}, u32[]{:S(2)}) collective-permute-start(f32[3,1,8,640]{3,2,0,1:T(8,128)S(1)} %bitcast.563), channel_id=1, source_target_pairs={{8,0},{16,8},{24,16},{32,24},{40,32},{48,40},{56,48},{64,56},{72,6... | collective-permute-start | bytes 184328 | tf_op jit(solution)/shard_map/ppermute | solution.py:36
  124.0 7.3 %collective-permute-start.4 = (f32[3,1,8,640]{3,2,0,1:T(8,128)S(1)}, f32[3,1,8,640]{3,2,0,1:T(8,128)S(1)}, u32[]{:S(2)}, u32[]{:S(2)}) collective-permute-start(f32[3,1,8,640]{3,2,0,1:T(8,128)S(1)} %bitcast.564), channel_id=1, source_target_pairs={{0,8},{8,16},{16,24},{24,32},{32,40},{40,48},{48,56},{56,64},{64,7... | collective-permute-start | bytes 184328 | tf_op jit(solution)/shard_map/ppermute | solution.py:35
  144.9 9.7 %all-to-all-start.8 = ((f32[8,1,7]{2,1,0:T(1,128)}), f32[8,1,7]{2,1,0:T(1,128)S(1)}, u32[]{:S(2)}, u32[]{:S(2)}) async-start(f32[8,1,7]{2,1,0:T(1,128)} %broadcast_in_dim.130), calls=%async_computation.8 | async-start | bytes 8192 | tf_op jit(solution)/shard_map/all_to_all | solution.py:21
  155.3 10.6 %all-to-all-start.7 = ((f32[8,3,1,1,640]{4,3,2,1,0:T(1,128)}), f32[8,3,1,1,640]{4,3,2,1,0:T(1,128)S(1)}, u32[]{:S(2)}, u32[]{:S(2)}) async-start(f32[8,3,1,1,640]{4,3,2,1,0:T(1,128)} %broadcast_in_dim.128), calls=%async_computation.7 | async-start | bytes 122880 | tf_op jit(solution)/shard_map/all_to_all | solution.py:21
  166.4 21.1 %all-to-all-start.9 = ((f32[64,1,7]{2,1,0:T(1,128)}), f32[64,1,7]{2,1,0:T(1,128)S(1)}, u32[]{:S(2)}, u32[]{:S(2)}) async-start(f32[64,1,7]{2,1,0:T(1,128)} %broadcast_in_dim.131), calls=%async_computation.9 | async-start | bytes 65536 | tf_op jit(solution)/shard_map/all_to_all | solution.py:21
  178.2 9.7 %collective-permute-start.7 = (f32[3,1,8,640]{3,2,0,1:T(8,128)S(1)}, f32[3,1,8,640]{3,2,0,1:T(8,128)S(1)}, u32[]{:S(2)}, u32[]{:S(2)}) collective-permute-start(f32[3,1,8,640]{3,2,0,1:T(8,128)S(1)} %bitcast.559), channel_id=1, source_target_pairs={{8,0},{16,8},{24,16},{32,24},{40,32},{48,40},{56,48},{64,56},{72,6... | collective-permute-start | bytes 184328 | tf_op jit(solution)/shard_map/ppermute | solution.py:36
  180.6 7.3 %collective-permute-start.6 = (f32[3,1,8,640]{3,2,0,1:T(8,128)S(1)}, f32[3,1,8,640]{3,2,0,1:T(8,128)S(1)}, u32[]{:S(2)}, u32[]{:S(2)}) collective-permute-start(f32[3,1,8,640]{3,2,0,1:T(8,128)S(1)} %bitcast.560), channel_id=1, source_target_pairs={{0,8},{8,16},{16,24},{24,32},{32,40},{40,48},{48,56},{56,64},{64,7... | collective-permute-start | bytes 184328 | tf_op jit(solution)/shard_map/ppermute | solution.py:35
where the time goes:
time: 203 us; the launch traced here: 200 us
  starting transfers between devices  90.3 us (44%)
  waiting for transfers between devices  56 us (28%)
  other arithmetic  30.5 us (15%)
  local copies, waits for them, and re-layouts  20.5 us (10%)
    all_to_all x10, starting transfers between devices, copy_for_each(): return lax.all_to_all(copies, axis, split_axis=0, concat_axis=0, tiled=True)  67.5 us
    all_to_all x10, waiting for transfers between devices, copy_for_each(): return lax.all_to_all(copies, axis, split_axis=0, concat_axis=0, tiled=True)  56 us
    ppermute x4, starting transfers between devices, with_halo(): before = lax.ppermute(last, axis, up)  11.9 us
    ppermute x4, starting transfers between devices, with_halo(): after = lax.ppermute(initial, axis, down)  10.8 us
    reduce_sum x12, other arithmetic, dipole_field(): jnp.sum(radial * delta_x - moments[0][None, :] * direct, axis=1)  10.7 us
    broadcast_in_dim x10, local copies, waits for them, and re-layouts, copy_for_each(): copies = jnp.broadcast_to(x, (lax.axis_size(axis), *x.shape))  6.27 us
    gather x10, local copies, waits for them, and re-layouts, listed_tiles(): taken = jnp.take(tile_set, index_lists, axis=1)  5.42 us
    reduce_sum x9, other arithmetic, dipole_potential(): return jnp.sum(projected * inv_cube, axis=1)  4.73 us
  transfers between devices with their start and end apart: 18, of which 10 were waited for; matrix products, arithmetic and copies ran while one was open for 2% of the time, Pallas kernels for 0%

commit v1 on v0

v1 whole, which is shorter than its diff:
```python
import functools

import jax
import jax.numpy as jnp
from jax import lax
from jax.experimental import pallas as pl
from jax.experimental.pallas import tpu as pltpu
from jax.sharding import Mesh, PartitionSpec as P

LANES = 128
ITERS = 3
SOFT = 0.04
X, Z, CORES, GROUPS = 4, 8, 2, 8
CHIPS = X * Z
MEMBERS = CORES * GROUPS
AB, GB = 4, 3
DYN = 16
FIRST = 40
SITE, POINT = 16, 28
OWN = 48
FIXED, POL, BASE, RESP = 21, 33, 37, 40

VM = pl.BlockSpec(memory_space=pltpu.VMEM)
SM = pl.BlockSpec(memory_space=pltpu.SMEM)


def out(*shape):
    return jax.ShapeDtypeStruct(shape, jnp.float32)


def call(kernel, outs, args, specs=None, flops=1_000_000, scratch=(), limit=8 << 20, name=None):
    return pl.pallas_call(
        kernel,
        out_shape=outs,
        in_specs=specs or [VM] * len(args),
        out_specs=jax.tree.map(lambda _: VM, outs),
        scratch_shapes=list(scratch),
        cost_estimate=pl.CostEstimate(flops=flops, bytes_accessed=1000, transcendentals=0),
        compiler_params=pltpu.CompilerParams(vmem_limit_bytes=limit),
        name=name,
    )(*args)


def block(ref, a, b):
    return ref[a : a + 1, b * LANES : (b + 1) * LANES]


def flat_block(ref, b):
    return ref[0:1, b * LANES : (b + 1) * LANES]


def begin_kernel(sites, points, guess, fixed, pol, base, resp, own, copies, rows):
    rows[...] = jnp.zeros_like(rows)
    own[...] = jnp.zeros_like(own)
    for b in range(AB):
        for a in range(3):
            rows[a * AB + b : a * AB + b + 1, :] = block(guess, a, b)
            s = block(sites, a, b)
            rows[SITE + a * AB + b : SITE + a * AB + b + 1, :] = s
            own[a * AB + b : a * AB + b + 1, :] = s
            own[FIXED + a * AB + b : FIXED + a * AB + b + 1, :] = block(fixed, a, b)
        own[POL + b : POL + b + 1, :] = flat_block(pol, b)
    for b in range(GB):
        for a in range(3):
            s = block(points, a, b)
            rows[POINT + a * GB + b : POINT + a * GB + b + 1, :] = s
            own[12 + a * GB + b : 12 + a * GB + b + 1, :] = s
        rows[12 + b : 13 + b, :] = flat_block(base, b)
        own[BASE + b : BASE + b + 1, :] = flat_block(base, b)
        own[RESP + b : RESP + b + 1, :] = flat_block(resp, b)
    everything = rows[...]
    for i in range(MEMBERS):
        copies[i] = everything


def position():
    core = lax.axis_index("core")
    return core, (lax.axis_index("x") * Z + lax.axis_index("z")) * CORES


def sums_kernel(dyn, static, far, halo, table):
    core, first_cell = position()
    table[...] = jnp.zeros_like(table)
    for k in range(CORES):
        dipoles = [jnp.zeros((AB, LANES), jnp.float32) for _ in range(3)]
        charge = jnp.zeros((GB, LANES), jnp.float32)
        offset = [jnp.zeros((GB, LANES), jnp.float32) for _ in range(3)]
        centre = [(first_cell + k).astype(jnp.float32) + 0.5, 0.5, 0.5]
        for g in range(GROUPS):
            m = k * GROUPS + g
            q = dyn[m, 12 : 12 + GB, :]
            charge = charge + q
            for a in range(3):
                dipoles[a] = dipoles[a] + dyn[m, a * AB : (a + 1) * AB, :]
                p = static[m, POINT + a * GB : POINT + (a + 1) * GB, :]
                offset[a] = offset[a] + q * (p - centre[a])
        for a in range(3):
            p = jnp.sum(dipoles[a], axis=0, keepdims=True)
            table[k * 8 + a : k * 8 + a + 1, :] = p
            table[k * 8 + 4 + a : k * 8 + 5 + a, :] = p + jnp.sum(offset[a], axis=0, keepdims=True)
        table[k * 8 + 3 : k * 8 + 4, :] = jnp.sum(charge, axis=0, keepdims=True)
    totals = jnp.broadcast_to(jnp.sum(table[...], axis=1, keepdims=True), (16, LANES))
    diagonal = lax.broadcasted_iota(jnp.int32, (16, LANES), 0) == lax.broadcasted_iota(
        jnp.int32, (16, LANES), 1
    )
    row = jnp.sum(jnp.where(diagonal, totals, 0.0), axis=0, keepdims=True)
    for i in range(CHIPS):
        far[i] = row
    halo[...] = dyn[pl.ds(core * GROUPS, GROUPS)]


def geometry(t, s):
    dx, dy, dz = (t[a] - s[a] for a in range(3))
    inverse = lax.rsqrt(dx * dx + dy * dy + (dz * dz + SOFT))
    square = inverse * inverse
    return dx, dy, dz, inverse * square, square


CHUNK = 32


def near_kernel(
    near, grids, sources, own, dyn, dyn_halo, static, static_halo, result, columns, sums, moving, fixed
):
    core, _ = position()
    moving[0:MEMBERS] = dyn[:, 0:DYN, :]
    moving[MEMBERS:] = dyn_halo[:, 0:DYN, :]
    fixed[0:MEMBERS] = static[:, SITE:FIRST, :]
    fixed[MEMBERS:] = static_halo[:, SITE:FIRST, :]
    for r in range(3 * AB + 3 * GB):
        columns[r] = jnp.transpose(jnp.broadcast_to(own[r : r + 1, :], (LANES, LANES)))

    first, second, third = (
        jnp.where(core == 0, MEMBERS, 0),
        jnp.where(core == 0, 0, GROUPS),
        jnp.where(core == 0, GROUPS, MEMBERS),
    )

    def place(slot, blocks):
        per_cell = blocks * GROUPS
        cell = slot // per_cell
        inside = slot - cell * per_cell
        share = jnp.where(cell == 0, first, jnp.where(cell == 1, second, third))
        group = inside // blocks
        return share + group, inside - group * blocks

    def rows(ref, share, start, step):
        return [ref[share, pl.ds(start + a * step, 1), :] for a in range(3)]

    def dipole_terms(share, b):
        s = rows(fixed, share, b, AB)
        m = rows(moving, share, b, AB)
        return s, m, [3.0 * v for v in m]

    me = second + lax.axis_index("grp")

    def atom_chunk(step, carry):
        tb = step // (LANES // CHUNK)
        start = pl.multiple_of((step - tb * (LANES // CHUNK)) * CHUNK, CHUNK)
        t = [columns[a * AB + tb, pl.ds(start, CHUNK), :] for a in range(3)]
        acc = [jnp.zeros((CHUNK, LANES), jnp.float32) for _ in range(3)]
        for n in range(9):
            if n == 0:
                share, b = me, tb
            else:
                share, b = place(near[tb, n - 1], AB)
            s, m, m3 = dipole_terms(share, b)
            dx, dy, dz, cube, square = geometry(t, s)
            weight = (m3[0] * dx + m3[1] * dy + m3[2] * dz) * (cube * square)
            if n == 0:
                other = (
                    lax.broadcasted_iota(jnp.int32, (CHUNK, LANES), 0) + start
                ) != lax.broadcasted_iota(jnp.int32, (CHUNK, LANES), 1)
                cube = jnp.where(other, cube, 0.0)
                weight = jnp.where(other, weight, 0.0)
            acc = [acc[a] + (weight * d - m[a] * cube) for a, d in enumerate((dx, dy, dz))]
        for n in range(4):
            share, b = place(grids[tb, n], GB)
            s = rows(fixed, share, 12 + b, GB)
            q = moving[share, pl.ds(12 + b, 1), :]
            dx, dy, dz, cube, _ = geometry(t, s)
            weight = q * cube
            acc = [acc[a] + weight * d for a, d in enumerate((dx, dy, dz))]
        for a in range(3):
            sums[a * AB + tb, pl.ds(start, CHUNK), :] = acc[a]
        return carry

    def grid_chunk(step, carry):
        tb = step // (LANES // CHUNK)
        start = pl.multiple_of((step - tb * (LANES // CHUNK)) * CHUNK, CHUNK)
        t = [columns[12 + a * GB + tb, pl.ds(start, CHUNK), :] for a in range(3)]
        acc = jnp.zeros((CHUNK, LANES), jnp.float32)
        for n in range(8):
            share, b = place(sources[tb, n], AB)
            s = rows(fixed, share, b, AB)
            m = rows(moving, share, b, AB)
            dx, dy, dz, cube, _ = geometry(t, s)
            acc = acc + (m[0] * dx + m[1] * dy + m[2] * dz) * cube
        sums[12 + tb, pl.ds(start, CHUNK), :] = acc
        return carry

    lax.fori_loop(0, AB * (LANES // CHUNK), atom_chunk, 0)
    lax.fori_loop(0, GB * (LANES // CHUNK), grid_chunk, 0)
    for r in range(12 + GB):
        result[r : r + 1, :] = jnp.sum(jnp.transpose(sums[r]), axis=0, keepdims=True)
    result[15:16, :] = jnp.zeros((1, LANES), jnp.float32)


def far_terms(table, here, targets):
    totals = [[jnp.zeros((8, LANES), jnp.float32) for _ in range(4)] for _ in range(AB)]
    potential = [jnp.zeros((8, LANES), jnp.float32) for _ in range(GB)]
    for k in range(CORES):
        for v in range(CHIPS // 8):
            chip = lax.broadcasted_iota(jnp.int32, (8, LANES), 0) + v * 8
            cell = chip * CORES + k
            centre = cell.astype(jnp.float32) + 0.5
            mask = jnp.where(jnp.abs(cell - here) >= 2, 1.0, 0.0)
            part = table[v * 8 : (v + 1) * 8, :]
            p0, p1, p2, q, m0, m1, m2 = (
                jnp.broadcast_to(part[:, k * 8 + j : k * 8 + j + 1], (8, LANES)) for j in range(7)
            )
            for b in range(AB):
                x, dy, dz = targets[b]
                dx = x - centre
                inverse = lax.rsqrt(dx * dx + (dy * dy + (dz * dz + SOFT)))
                square = inverse * inverse
                cube = inverse * square * mask
                weight = 3.0 * (m0 * dx + m1 * dy + m2 * dz) * (cube * square) + q * cube
                acc = totals[b]
                totals[b] = [
                    acc[0] + (weight * dx - m0 * cube),
                    acc[1] + m1 * cube,
                    acc[2] + m2 * cube,
                    acc[3] + weight,
                ]
            for b in range(GB):
                x, dy, dz = targets[AB + b]
                dx = x - centre
                inverse = lax.rsqrt(dx * dx + (dy * dy + (dz * dz + SOFT)))
                cube = inverse * (inverse * inverse) * mask
                potential[b] = potential[b] + (p0 * dx + p1 * dy + p2 * dz) * cube
    fields = []
    for b in range(AB):
        _, dy, dz = targets[b]
        sx, sy, sz, sw = (jnp.sum(t, axis=0, keepdims=True) for t in totals[b])
        fields.append((sx, dy * sw - sy, dz * sw - sz))
    return fields, [jnp.sum(p, axis=0, keepdims=True) for p in potential]


def update_kernel(last, own, near, far, *refs):
    core, first_cell = position()
    targets = []
    for b in range(AB):
        targets.append((own[b : b + 1, :], own[AB + b : AB + b + 1, :] - 0.5, own[2 * AB + b : 2 * AB + b + 1, :] - 0.5))
    for b in range(GB):
        r = 12 + b
        targets.append((own[r : r + 1, :], own[r + GB : r + GB + 1, :] - 0.5, own[r + 2 * GB : r + 2 * GB + 1, :] - 0.5))
    fields, potential = far_terms(far[:, 0, :], first_cell + core, targets)
    if last:
        dipoles, charges = refs
    else:
        copies, rows = refs
        rows[15:16, :] = jnp.zeros((1, LANES), jnp.float32)
    for b in range(AB):
        pol = own[POL + b : POL + b + 1, :]
        for a in range(3):
            r = a * AB + b
            value = pol * (own[FIXED + r : FIXED + r + 1, :] + (near[r : r + 1, :] + fields[b][a]))
            if last:
                dipoles[a : a + 1, b * LANES : (b + 1) * LANES] = value
            else:
                rows[r : r + 1, :] = value
    for b in range(GB):
        value = own[BASE + b : BASE + b + 1, :] - own[RESP + b : RESP + b + 1, :] * (
            near[12 + b : 13 + b, :] + potential[b]
        )
        if last:
            charges[0:1, b * LANES : (b + 1) * LANES] = value
        else:
            rows[12 + b : 13 + b, :] = value
    if not last:
        everything = rows[...]
        for i in range(MEMBERS):
            copies[i] = everything


def swaps():
    pairs = []
    for c in range(1, CHIPS * CORES - 1, 2):
        for g in range(GROUPS):
            i, j = c * GROUPS + g, (c + 1) * GROUPS + g
            pairs += [(i, j), (j, i)]
    return pairs


def body(sites, points, guess, fixed, pol, base, resp, near, grids, sources):
    flat = lambda v: v.reshape(1, -1)
    own, copies = call(
        begin_kernel,
        (out(OWN, LANES), out(MEMBERS, FIRST, LANES)),
        (sites, points, guess, fixed, flat(pol), flat(base), flat(resp)),
        scratch=[pltpu.VMEM((FIRST, LANES), jnp.float32)],
        name="begin",
    )
    static = static_halo = None
    for iteration in range(ITERS):
        last = iteration == ITERS - 1
        height = FIRST if iteration == 0 else DYN
        dyn = lax.all_to_all(copies, ("core", "grp"), 0, 0, tiled=True)
        static = dyn if static is None else static
        far_out, halo_out = call(
            sums_kernel,
            (out(CHIPS, 1, LANES), out(GROUPS, height, LANES)),
            (dyn, static),
            scratch=[pltpu.VMEM((16, LANES), jnp.float32)],
            name="sums",
        )
        halo = lax.ppermute(halo_out, ("x", "z", "core", "grp"), swaps())
        far = lax.all_to_all(far_out, ("x", "z"), 0, 0, tiled=True)
        static_halo = halo if static_halo is None else static_halo
        near_field = call(
            near_kernel,
            out(16, LANES),
            (near, grids, sources, own, dyn, halo, static, static_halo),
            specs=[SM] * 3 + [VM] * 5,
            flops=40_000_000,
            scratch=[
                pltpu.VMEM((21, LANES, LANES), jnp.float32),
                pltpu.VMEM((15, LANES, LANES), jnp.float32),
                pltpu.VMEM((MEMBERS + GROUPS, DYN, LANES), jnp.float32),
                pltpu.VMEM((MEMBERS + GROUPS, FIRST - SITE, LANES), jnp.float32),
            ],
            limit=16 << 20,
            name="near",
        )
        if last:
            dipoles, charges = call(
                functools.partial(update_kernel, True),
                (out(3, AB * LANES), out(1, GB * LANES)),
                (own, near_field, far),
                name="finish",
            )
        else:
            copies = call(
                functools.partial(update_kernel, False),
                out(MEMBERS, DYN, LANES),
                (own, near_field, far),
                scratch=[pltpu.VMEM((DYN, LANES), jnp.float32)],
                name="update",
            )
    return dipoles, charges.reshape(-1)


def solution(mesh):
    fine = Mesh(mesh.devices.reshape(X, Z, CORES, GROUPS), ("x", "z", "core", "grp"))
    every = ("x", "z", "core", "grp")
    return jax.shard_map(
        body,
        mesh=fine,
        in_specs=(P(None, every),) * 4 + (P(every),) * 3 + (P(every, None),) * 3,
        out_specs=(P(None, every), P(every)),
        check_vma=False,
    )
```

time: 203 us -> 121 us (0.60)
  waiting for transfers between devices: 56 us -> 3.13 us
  starting transfers between devices: 90.3 us -> 38.1 us
  blocking collectives: 0 us -> 43.4 us
  Pallas kernels: 0 us -> 29.9 us
  other arithmetic: 30.5 us -> 0.6 us
  local copies, waits for them, and re-layouts: 20.5 us -> 4.16 us
    all_to_all x10 -> x3, waiting for transfers between devices: 56 us -> 3.13 us  [body(): far = lax.all_to_all(far_out, ('x', 'z'), 0, 0, tiled=True)]
    all_to_all x0 -> x3, blocking collectives: none -> 43.4 us  [body(): dyn = lax.all_to_all(copies, ('core', 'grp'), 0, 0, tiled=True)]
    all_to_all x10 -> x3, starting transfers between devices: 67.5 us -> 27.2 us  [body(): far = lax.all_to_all(far_out, ('x', 'z'), 0, 0, tiled=True)]
    pallas_call x0 -> x10, Pallas kernels: none -> 29.9 us  [call(): pl.pallas_call(kernel, out_shape=outs, in_specs=specs or [VM] * len(args)...]
    reduce_sum x66 -> x0, other arithmetic: 25.1 us -> none  [the longest x12 10.7 us: dipole_field(): jnp.sum(radial * delta_x - moments[0][None, :] * direct, axis=1)]
    ppermute x8 -> x3, starting transfers between devices: 22.7 us -> 10.9 us  [body(): halo = lax.ppermute(halo_out, ('x', 'z', 'core', 'grp'), swaps())]
    gather x13 -> x0, local copies, waits for them, and re-layouts: 7.11 us -> none  [the longest x10 5.42 us: listed_tiles(): taken = jnp.take(tile_set, index_lists, axis=1)]
    broadcast_in_dim x13 -> x0, local copies, waits for them, and re-layouts: 6.52 us -> none  [the longest x10 6.27 us: copy_for_each(): copies = jnp.broadcast_to(x, (lax.axis_size(axis), *x.shape))]
  transfers between devices with their start and end apart: 18 -> 6, of which waited for: 10 -> 3; matrix products, arithmetic and copies ran while one was open for 2% -> 0% of each run, Pallas kernels for 0% -> 19%
where the time goes in v1:
time: 121 us; the launch traced here: 120 us
  blocking collectives  43.4 us (36%)
  starting transfers between devices  38.1 us (31%)
  Pallas kernels  29.9 us (25%)
  local copies, waits for them, and re-layouts  4.16 us (3%)
  waiting for transfers between devices  3.13 us (3%)
    all_to_all x3, blocking collectives, body(): dyn = lax.all_to_all(copies, ('core', 'grp'), 0, 0, tiled=True)  43.4 us
    pallas_call x10, Pallas kernels, call(): pl.pallas_call(kernel, out_shape=outs, in_specs=specs or [VM] * len(args)...  29.9 us
    all_to_all x3, starting transfers between devices, body(): far = lax.all_to_all(far_out, ('x', 'z'), 0, 0, tiled=True)  27.2 us
    ppermute x3, starting transfers between devices, body(): halo = lax.ppermute(halo_out, ('x', 'z', 'core', 'grp'), swaps())  10.9 us
    all_to_all x3, waiting for transfers between devices, body(): far = lax.all_to_all(far_out, ('x', 'z'), 0, 0, tiled=True)  3.13 us
    unnamed x16, local copies, waits for them, and re-layouts  2.79 us
  transfers between devices with their start and end apart: 6, of which 3 were waited for; matrix products, arithmetic and copies ran while one was open for 0% of the time, Pallas kernels for 19%

profile of v1, /device:TPU:1, one launch (start us, length us, event | category | flops | bytes accessed | tf_op | source)
XLA Modules:
  0.0 120.0 jit_solution(17902403618000448866)
XLA Ops:
  0.6 0.0 copy-start.3
  0.6 0.7 reshape.17.base
  1.3 0.7 reshape.18.resp
  2.0 0.0 copy-done.3
  2.0 0.0 copy-start.4
  2.0 0.7 copy-done.4
  2.7 0.0 copy-start.5
  2.7 0.7 copy-done.5
  3.4 0.0 copy-start.6
  3.4 0.7 copy-done.6
  4.1 0.0 copy-start.7
  4.1 0.7 copy-done.7
  4.8 20.1 %all_to_all.30.dyn.static = f32[16,40,128]{2,1,0:T(8,128)S(1)} all-to-all(f32[16,40,128]{2,1,0:T(8,128)S(1)} %get-tuple-element.13), channel_id=1, replica_groups=mesh['x'=4,'z'=8,'core'=2,'grp'=8] {'core','grp'}, dimensions={0} | all-to-all | bytes 655360 | tf_op jit(solution)/shard_map/all_to_all | solution.py:309
  24.9 0.7 sums.3
  25.6 4.2 %collective-permute-start = (f32[8,40,128]{2,1,0:T(8,128)S(1)}, f32[8,40,128]{2,1,0:T(8,128)S(1)}, u32[]{:S(2)}, u32[]{:S(2)}) collective-permute-start(f32[8,40,128]{2,1,0:T(8,128)S(1)} %get-tuple-element.14), channel_id=1, source_target_pairs={{8,16},{16,8},{9,17},{17,9},{10,18},{18,10},{11,19},{19,11},{12,20... | collective-permute-start | bytes 491528 | tf_op jit(solution)/shard_map/ppermute | solution.py:318
  29.8 0.0 copy-start
  29.8 0.0 copy-start.1
  29.8 0.0 copy-start.2
  29.8 12.1 %all-to-all-start.1 = ((f32[32,1,128]{2,1,0:T(1,128)}), f32[32,1,128]{2,1,0:T(1,128)S(1)}, u32[]{:S(2)}, u32[]{:S(2)}) async-start(f32[32,1,128]{2,1,0:T(1,128)} %get-tuple-element.15), calls=%async_computation.1 | async-start | bytes 32768 | tf_op jit(solution)/shard_map/all_to_all | solution.py:319
  42.0 0.0 collective-permute-done.dyn_halo.static_halo
  42.0 0.0 copy-done
  42.0 0.0 copy-done.1
  42.0 0.0 copy-done.2
  42.0 7.6 %near.6 = f32[16,128]{1,0:T(8,128)S(1)} custom-call(s32[4,8]{1,0:T(4,128)S(1)} %copy-done, s32[4,4]{1,0:T(4,128)S(1)} %copy-done.1, s32[3,8]{1,0:T(4,128)S(1)} %copy-done.2, f32[48,128]{1,0:T(8,128)S(1)} %get-tuple-element.12.own, f32[16,40,128]{2,1,0:T(8,128)S(1)} %all_to_all.30.dyn.static, f32[8,40,128]{2,1,0:T(8,128)S(1)} %collective-permute-done.dyn_halo.static_halo, ...), custom_call_target="tpu_custom_call" | custom-call | flops 40000000 | bytes 1000 | tf_op jit(solution)/shard_map/near/pallas_call | solution.py:32
  49.6 1.0 all-to-all-done.1.far
  50.6 1.4 %update.2 = f32[16,16,128]{2,1,0:T(8,128)S(1)} custom-call(f32[48,128]{1,0:T(8,128)S(1)} %get-tuple-element.12.own, f32[16,128]{1,0:T(8,128)S(1)} %near.6, f32[32,1,128]{2,1,0:T(1,128)S(1)} %all-to-all-done.1.far), custom_call_target="tpu_custom_call" | custom-call | flops 1000000 | bytes 1000 | tf_op jit(solution)/shard_map/update/pallas_call | solution.py:32
  52.0 11.7 %all_to_all.31.dyn = f32[16,16,128]{2,1,0:T(8,128)S(1)} all-to-all(f32[16,16,128]{2,1,0:T(8,128)S(1)} %update.2), channel_id=1, replica_groups=mesh['x'=4,'z'=8,'core'=2,'grp'=8] {'core','grp'}, dimensions={0} | all-to-all | bytes 262144 | tf_op jit(solution)/shard_map/all_to_all | solution.py:309
  63.8 0.7 sums.4
  64.5 3.4 %collective-permute-start.1 = (f32[8,16,128]{2,1,0:T(8,128)S(1)}, f32[8,16,128]{2,1,0:T(8,128)S(1)}, u32[]{:S(2)}, u32[]{:S(2)}) collective-permute-start(f32[8,16,128]{2,1,0:T(8,128)S(1)} %get-tuple-element.16), channel_id=1, source_target_pairs={{8,16},{16,8},{9,17},{17,9},{10,18},{18,10},{11,19},{19,11},{12,20... | collective-permute-start | bytes 196616 | tf_op jit(solution)/shard_map/ppermute | solution.py:318
  67.9 7.8 %all-to-all-start.3 = ((f32[32,1,128]{2,1,0:T(1,128)}), f32[32,1,128]{2,1,0:T(1,128)S(1)}, u32[]{:S(2)}, u32[]{:S(2)}) async-start(f32[32,1,128]{2,1,0:T(1,128)} %get-tuple-element.17), calls=%async_computation.3 | async-start | bytes 32768 | tf_op jit(solution)/shard_map/all_to_all | solution.py:319
  75.7 0.0 collective-permute-done.1.dyn_halo
  75.7 7.6 %near.8 = f32[16,128]{1,0:T(8,128)S(1)} custom-call(s32[4,8]{1,0:T(4,128)S(1)} %copy-done, s32[4,4]{1,0:T(4,128)S(1)} %copy-done.1, s32[3,8]{1,0:T(4,128)S(1)} %copy-done.2, f32[48,128]{1,0:T(8,128)S(1)} %get-tuple-element.12.own, f32[16,16,128]{2,1,0:T(8,128)S(1)} %all_to_all.31.dyn, f32[8,16,128]{2,1,0:T(8,128)S(1)} %collective-permute-done.1.dyn_halo, ...), custom_call_target="tpu_custom_call" | custom-call | flops 40000000 | bytes 1000 | tf_op jit(solution)/shard_map/near/pallas_call | solution.py:32
  83.3 1.1 all-to-all-done.3.far
  84.3 1.4 %update.3 = f32[16,16,128]{2,1,0:T(8,128)S(1)} custom-call(f32[48,128]{1,0:T(8,128)S(1)} %get-tuple-element.12.own, f32[16,128]{1,0:T(8,128)S(1)} %near.8, f32[32,1,128]{2,1,0:T(1,128)S(1)} %all-to-all-done.3.far), custom_call_target="tpu_custom_call" | custom-call | flops 1000000 | bytes 1000 | tf_op jit(solution)/shard_map/update/pallas_call | solution.py:32
  85.7 11.6 %all_to_all.32.dyn = f32[16,16,128]{2,1,0:T(8,128)S(1)} all-to-all(f32[16,16,128]{2,1,0:T(8,128)S(1)} %update.3), channel_id=1, replica_groups=mesh['x'=4,'z'=8,'core'=2,'grp'=8] {'core','grp'}, dimensions={0} | all-to-all | bytes 262144 | tf_op jit(solution)/shard_map/all_to_all | solution.py:309
  97.3 0.7 sums.5
  98.0 3.4 %collective-permute-start.2 = (f32[8,16,128]{2,1,0:T(8,128)S(1)}, f32[8,16,128]{2,1,0:T(8,128)S(1)}, u32[]{:S(2)}, u32[]{:S(2)}) collective-permute-start(f32[8,16,128]{2,1,0:T(8,128)S(1)} %get-tuple-element.18), channel_id=1, source_target_pairs={{8,16},{16,8},{9,17},{17,9},{10,18},{18,10},{11,19},{19,11},{12,20... | collective-permute-start | bytes 196616 | tf_op jit(solution)/shard_map/ppermute | solution.py:318
  101.4 7.3 %all-to-all-start.5 = ((f32[32,1,128]{2,1,0:T(1,128)}), f32[32,1,128]{2,1,0:T(1,128)S(1)}, u32[]{:S(2)}, u32[]{:S(2)}) async-start(f32[32,1,128]{2,1,0:T(1,128)} %get-tuple-element.19), calls=%async_computation.5 | async-start | bytes 32768 | tf_op jit(solution)/shard_map/all_to_all | solution.py:319
  108.7 0.0 collective-permute-done.2.dyn_halo
  108.7 7.6 %near.10 = f32[16,128]{1,0:T(8,128)S(1)} custom-call(s32[4,8]{1,0:T(4,128)S(1)} %copy-done, s32[4,4]{1,0:T(4,128)S(1)} %copy-done.1, s32[3,8]{1,0:T(4,128)S(1)} %copy-done.2, f32[48,128]{1,0:T(8,128)S(1)} %get-tuple-element.12.own, f32[16,16,128]{2,1,0:T(8,128)S(1)} %all_to_all.32.dyn, f32[8,16,128]{2,1,0:T(8,128)S(1)} %collective-permute-done.2.dyn_halo, ...), custom_call_target="tpu_custom_call" | custom-call | flops 40000000 | bytes 1000 | tf_op jit(solution)/shard_map/near/pallas_call | solution.py:32
  116.3 1.1 all-to-all-done.5.far
  117.4 2.0 %finish.1 = (f32[3,512]{1,0:T(4,128)}, f32[1,384]{1,0:T(1,128)S(1)}) custom-call(f32[48,128]{1,0:T(8,128)S(1)} %get-tuple-element.12.own, f32[16,128]{1,0:T(8,128)S(1)} %near.10, f32[32,1,128]{2,1,0:T(1,128)S(1)} %all-to-all-done.5.far), custom_call_target="tpu_custom_call" | custom-call | flops 1000000 | bytes 1000 | tf_op jit(solution)/shard_map/finish/pallas_call | solution.py:32
  119.4 0.6 reduce
  (1 shorter events, 0.0 us)
Async XLA Ops:
  0.6 1.4 %copy-start.3 = (f32[3,512]{1,0:T(4,128)S(1)}, f32[3,512]{1,0:T(4,128)}, u32[]{:S(2)}) copy-start(f32[3,512]{1,0:T(4,128)} %sites.1) | copy-start | bytes 18436
  2.0 0.7 copy-start.4
  2.7 0.7 copy-start.5
  3.4 0.7 copy-start.6
  4.1 0.7 copy-start.7
  25.6 16.3 %collective-permute-start = (f32[8,40,128]{2,1,0:T(8,128)S(1)}, f32[8,40,128]{2,1,0:T(8,128)S(1)}, u32[]{:S(2)}, u32[]{:S(2)}) collective-permute-start(f32[8,40,128]{2,1,0:T(8,128)S(1)} %get-tuple-element.14), channel_id=1, source_target_pairs={{8,16},{16,8},{9,17},{17,9},{10,18},{18,10},{11,19},{19,11},{12,20... | collective-permute-start | bytes 491528 | tf_op jit(solution)/shard_map/ppermute | solution.py:318
  29.8 12.2 %copy-start = (s32[4,8]{1,0:T(4,128)S(1)}, s32[4,8]{1,0:T(4,128)}, u32[]{:S(2)}) copy-start(s32[4,8]{1,0:T(4,128)} %near.11) | copy-start | bytes 388
  29.8 12.2 %copy-start.1 = (s32[4,4]{1,0:T(4,128)S(1)}, s32[4,4]{1,0:T(4,128)}, u32[]{:S(2)}) copy-start(s32[4,4]{1,0:T(4,128)} %grids.5) | copy-start | bytes 196
  29.8 12.2 %copy-start.2 = (s32[3,8]{1,0:T(4,128)S(1)}, s32[3,8]{1,0:T(4,128)}, u32[]{:S(2)}) copy-start(s32[3,8]{1,0:T(4,128)} %sources.5) | copy-start | bytes 292
  29.8 20.8 %all-to-all-start.1 = ((f32[32,1,128]{2,1,0:T(1,128)}), f32[32,1,128]{2,1,0:T(1,128)S(1)}, u32[]{:S(2)}, u32[]{:S(2)}) async-start(f32[32,1,128]{2,1,0:T(1,128)} %get-tuple-element.15), calls=%async_computation.1 | async-start | bytes 32768 | tf_op jit(solution)/shard_map/all_to_all | solution.py:319
  64.5 11.2 %collective-permute-start.1 = (f32[8,16,128]{2,1,0:T(8,128)S(1)}, f32[8,16,128]{2,1,0:T(8,128)S(1)}, u32[]{:S(2)}, u32[]{:S(2)}) collective-permute-start(f32[8,16,128]{2,1,0:T(8,128)S(1)} %get-tuple-element.16), channel_id=1, source_target_pairs={{8,16},{16,8},{9,17},{17,9},{10,18},{18,10},{11,19},{19,11},{12,20... | collective-permute-start | bytes 196616 | tf_op jit(solution)/shard_map/ppermute | solution.py:318
  67.9 16.4 %all-to-all-start.3 = ((f32[32,1,128]{2,1,0:T(1,128)}), f32[32,1,128]{2,1,0:T(1,128)S(1)}, u32[]{:S(2)}, u32[]{:S(2)}) async-start(f32[32,1,128]{2,1,0:T(1,128)} %get-tuple-element.17), calls=%async_computation.3 | async-start | bytes 32768 | tf_op jit(solution)/shard_map/all_to_all | solution.py:319
  98.0 10.7 %collective-permute-start.2 = (f32[8,16,128]{2,1,0:T(8,128)S(1)}, f32[8,16,128]{2,1,0:T(8,128)S(1)}, u32[]{:S(2)}, u32[]{:S(2)}) collective-permute-start(f32[8,16,128]{2,1,0:T(8,128)S(1)} %get-tuple-element.18), channel_id=1, source_target_pairs={{8,16},{16,8},{9,17},{17,9},{10,18},{18,10},{11,19},{19,11},{12,20... | collective-permute-start | bytes 196616 | tf_op jit(solution)/shard_map/ppermute | solution.py:318
  101.4 15.9 %all-to-all-start.5 = ((f32[32,1,128]{2,1,0:T(1,128)}), f32[32,1,128]{2,1,0:T(1,128)S(1)}, u32[]{:S(2)}, u32[]{:S(2)}) async-start(f32[32,1,128]{2,1,0:T(1,128)} %get-tuple-element.19), calls=%async_computation.5 | async-start | bytes 32768 | tf_op jit(solution)/shard_map/all_to_all | solution.py:319

commit v2 on v1

v2 whole, which is shorter than its diff:
```python
import functools

import jax
import jax.numpy as jnp
from jax import lax
from jax.experimental import pallas as pl
from jax.experimental.pallas import tpu as pltpu
from jax.sharding import Mesh, PartitionSpec as P


LANES = 128
ITERS = 3
SOFT = 0.04
X, Z, CORES, GROUPS = 4, 8, 2, 8
CHIPS = X * Z
MEMBERS = CORES * GROUPS
AB, GB = 4, 3
DYN = 16
FIRST = 40
SITE, POINT = 16, 28
OWN = 48
FIXED, POL, BASE, RESP = 21, 33, 37, 40

VM = pl.BlockSpec(memory_space=pltpu.VMEM)
SM = pl.BlockSpec(memory_space=pltpu.SMEM)
ANY = pl.BlockSpec(memory_space=pl.ANY)


def out(*shape):
    return jax.ShapeDtypeStruct(shape, jnp.float32)


def call(kernel, outs, args, specs=None, flops=1_000_000, scratch=(), limit=8 << 20):
    return pl.pallas_call(
        kernel,
        out_shape=outs,
        in_specs=specs or [VM] * len(args),
        out_specs=jax.tree.map(lambda _: VM, outs),
        scratch_shapes=list(scratch),
        cost_estimate=pl.CostEstimate(flops=flops, bytes_accessed=1000, transcendentals=0),
        compiler_params=pltpu.CompilerParams(vmem_limit_bytes=limit),
    )(*args)


def share_sums(rows, own, table):
    core, first_cell = position()
    centre = [(first_cell + core).astype(jnp.float32) + 0.5, 0.5, 0.5]
    q = rows[12 : 12 + GB, :]
    table[7:8, :] = jnp.zeros((1, LANES), jnp.float32)
    table[3:4, :] = jnp.sum(q, axis=0, keepdims=True)
    for a in range(3):
        p = jnp.sum(rows[a * AB : (a + 1) * AB, :], axis=0, keepdims=True)
        d = q * (own[12 + a * GB : 12 + (a + 1) * GB, :] - centre[a])
        table[a : a + 1, :] = p
        table[4 + a : 5 + a, :] = p + jnp.sum(d, axis=0, keepdims=True)
    totals = jnp.broadcast_to(jnp.sum(table[...], axis=1, keepdims=True), (8, LANES))
    lane = lax.broadcasted_iota(jnp.int32, (8, LANES), 1)
    chosen = (lax.broadcasted_iota(jnp.int32, (8, LANES), 0) == (lane & 7)) & (lane < 16)
    rows[15:16, :] = jnp.sum(jnp.where(chosen, totals, 0.0), axis=0, keepdims=True)


def begin_kernel(
    sites, points, guess, fixed, pol, base, resp, own, copies, rows, table, in_sites, in_points, in_guess, in_fixed, sems
):
    pieces = [(sites, in_sites), (points, in_points), (guess, in_guess), (fixed, in_fixed)]
    for b in range(AB):
        pieces.append((pol.at[pl.ds(b * LANES, LANES)], own.at[POL + b]))
    for b in range(GB):
        pieces.append((base.at[pl.ds(b * LANES, LANES)], own.at[BASE + b]))
        pieces.append((resp.at[pl.ds(b * LANES, LANES)], own.at[RESP + b]))
    moves = [pltpu.make_async_copy(src, dst, sems.at[i]) for i, (src, dst) in enumerate(pieces)]
    for move in moves:
        move.start()
    rows[37:40, :] = jnp.zeros((3, LANES), jnp.float32)
    own[43:48, :] = jnp.zeros((5, LANES), jnp.float32)
    for move in moves:
        move.wait()
    for b in range(AB):
        lanes = slice(b * LANES, (b + 1) * LANES)
        for a in range(3):
            r = a * AB + b
            s = in_sites[a : a + 1, lanes]
            rows[r : r + 1, :] = in_guess[a : a + 1, lanes]
            rows[SITE + r : SITE + r + 1, :] = s
            own[r : r + 1, :] = s
            own[FIXED + r : FIXED + r + 1, :] = in_fixed[a : a + 1, lanes]
    for b in range(GB):
        lanes = slice(b * LANES, (b + 1) * LANES)
        for a in range(3):
            r = a * GB + b
            s = in_points[a : a + 1, lanes]
            rows[POINT + r : POINT + r + 1, :] = s
            own[12 + r : 13 + r, :] = s
        rows[12 + b : 13 + b, :] = own[BASE + b : BASE + b + 1, :]
    share_sums(rows, own, table)
    everything = rows[...]
    for i in range(MEMBERS):
        copies[i] = everything


def position():
    core = lax.axis_index("core")
    return core, (lax.axis_index("x") * Z + lax.axis_index("z")) * CORES


def sums_kernel(dyn, far, halo):
    core, _ = position()
    totals = []
    for k in range(CORES):
        total = dyn[k * GROUPS, 15:16, :]
        for g in range(1, GROUPS):
            total = total + dyn[k * GROUPS + g, 15:16, :]
        totals.append(total)
    lane = lax.broadcasted_iota(jnp.int32, (1, LANES), 1)
    row = jnp.where(lane < 8, totals[0], totals[1])
    for i in range(CHIPS):
        far[i] = row
    halo[...] = dyn[pl.ds(core * GROUPS, GROUPS)]


def geometry(t, s):
    dx, dy, dz = (t[a] - s[a] for a in range(3))
    inverse = lax.rsqrt(dx * dx + dy * dy + (dz * dz + SOFT))
    square = inverse * inverse
    return dx, dy, dz, inverse * square, square


CHUNK = 128


def near_kernel(
    near, grids, sources, own, dyn, dyn_halo, static, static_halo, result, columns, sums, moving, fixed
):
    core, _ = position()
    moving[0:MEMBERS] = dyn[:, 0:DYN, :]
    moving[MEMBERS:] = dyn_halo[:, 0:DYN, :]
    fixed[0:MEMBERS] = static[:, SITE:FIRST, :]
    fixed[MEMBERS:] = static_halo[:, SITE:FIRST, :]
    for r in range(3 * AB + 3 * GB):
        columns[r] = jnp.transpose(jnp.broadcast_to(own[r : r + 1, :], (LANES, LANES)))

    first, second, third = (
        jnp.where(core == 0, MEMBERS, 0),
        jnp.where(core == 0, 0, GROUPS),
        jnp.where(core == 0, GROUPS, MEMBERS),
    )

    def place(slot, blocks):
        per_cell = blocks * GROUPS
        cell = slot // per_cell
        inside = slot - cell * per_cell
        share = jnp.where(cell == 0, first, jnp.where(cell == 1, second, third))
        group = inside // blocks
        return share + group, inside - group * blocks

    def rows(ref, share, start, step):
        return [ref[share, pl.ds(start + a * step, 1), :] for a in range(3)]

    def dipole_terms(share, b):
        s = rows(fixed, share, b, AB)
        m = rows(moving, share, b, AB)
        return s, m, [3.0 * v for v in m]

    me = second + lax.axis_index("grp")

    def atom_chunk(step, carry):
        tb = step // (LANES // CHUNK)
        start = pl.multiple_of((step - tb * (LANES // CHUNK)) * CHUNK, CHUNK)
        t = [columns[a * AB + tb, pl.ds(start, CHUNK), :] for a in range(3)]
        acc = [jnp.zeros((CHUNK, LANES), jnp.float32) for _ in range(3)]
        for n in range(9):
            if n == 0:
                share, b = me, tb
            else:
                share, b = place(near[tb, n - 1], AB)
            s, m, m3 = dipole_terms(share, b)
            dx, dy, dz, cube, square = geometry(t, s)
            weight = (m3[0] * dx + m3[1] * dy + m3[2] * dz) * (cube * square)
            if n == 0:
                other = (
                    lax.broadcasted_iota(jnp.int32, (CHUNK, LANES), 0) + start
                ) != lax.broadcasted_iota(jnp.int32, (CHUNK, LANES), 1)
                cube = jnp.where(other, cube, 0.0)
                weight = jnp.where(other, weight, 0.0)
            acc = [acc[a] + (weight * d - m[a] * cube) for a, d in enumerate((dx, dy, dz))]
        for n in range(4):
            share, b = place(grids[tb, n], GB)
            s = rows(fixed, share, 12 + b, GB)
            q = moving[share, pl.ds(12 + b, 1), :]
            dx, dy, dz, cube, _ = geometry(t, s)
            weight = q * cube
            acc = [acc[a] + weight * d for a, d in enumerate((dx, dy, dz))]
        for a in range(3):
            sums[a * AB + tb, pl.ds(start, CHUNK), :] = acc[a]
        return carry

    def grid_chunk(step, carry):
        tb = step // (LANES // CHUNK)
        start = pl.multiple_of((step - tb * (LANES // CHUNK)) * CHUNK, CHUNK)
        t = [columns[12 + a * GB + tb, pl.ds(start, CHUNK), :] for a in range(3)]
        acc = jnp.zeros((CHUNK, LANES), jnp.float32)
        for n in range(8):
            share, b = place(sources[tb, n], AB)
            s = rows(fixed, share, b, AB)
            m = rows(moving, share, b, AB)
            dx, dy, dz, cube, _ = geometry(t, s)
            acc = acc + (m[0] * dx + m[1] * dy + m[2] * dz) * cube
        sums[12 + tb, pl.ds(start, CHUNK), :] = acc
        return carry

    lax.fori_loop(0, AB * (LANES // CHUNK), atom_chunk, 0)
    lax.fori_loop(0, GB * (LANES // CHUNK), grid_chunk, 0)
    for r in range(12 + GB):
        result[r : r + 1, :] = jnp.sum(jnp.transpose(sums[r]), axis=0, keepdims=True)
    result[15:16, :] = jnp.zeros((1, LANES), jnp.float32)


VECTORS = CORES * CHIPS // 8


def far_terms(far, table, wide, here, own):
    for i in range(CHIPS):
        table[i : i + 1, :] = far[i]
    centres, masks = [], []
    for n in range(VECTORS):
        k, v = n // (CHIPS // 8), n % (CHIPS // 8)
        cell = (lax.broadcasted_iota(jnp.int32, (8, LANES), 0) + v * 8) * CORES + k
        centres.append(cell.astype(jnp.float32) + 0.5)
        masks.append(jnp.where(jnp.abs(cell - here) >= 2, 1.0, 0.0))
        part = table[v * 8 : (v + 1) * 8, :]
        for j in range(7):
            wide[n * 7 + j] = jnp.broadcast_to(part[:, k * 8 + j : k * 8 + j + 1], (8, LANES))

    def wide_row(r):
        return jnp.broadcast_to(own[r : r + 1, :], (8, LANES))

    fields, potential = [], []
    for b in range(AB + GB):
        atom = b < AB
        r, stride = (b, AB) if atom else (12 + b - AB, GB)
        x, dy, dz = wide_row(r), wide_row(r + stride) - 0.5, wide_row(r + 2 * stride) - 0.5
        across = dy * dy + (dz * dz + SOFT)
        sums = None
        for n in range(VECTORS):
            dx = x - centres[n]
            inverse = lax.rsqrt(dx * dx + across)
            square = inverse * inverse
            cube = inverse * square * masks[n]
            if atom:
                q, m0, m1, m2 = (wide[n * 7 + j] for j in (3, 4, 5, 6))
                weight = 3.0 * (m0 * dx + m1 * dy + m2 * dz) * (cube * square) + q * cube
                terms = [weight * dx - m0 * cube, m1 * cube, m2 * cube, weight]
            else:
                p0, p1, p2 = (wide[n * 7 + j] for j in (0, 1, 2))
                terms = [(p0 * dx + p1 * dy + p2 * dz) * cube]
            sums = terms if sums is None else [s + t for s, t in zip(sums, terms)]
        if atom:
            sx, sy, sz, sw = sums
            parts = [sx, dy * sw - sy, dz * sw - sz]
            fields.append([jnp.sum(t, axis=0, keepdims=True) for t in parts])
        else:
            potential.append(jnp.sum(sums[0], axis=0, keepdims=True))
    return fields, potential


def update_kernel(last, own, near, far, *refs):
    core, first_cell = position()
    if last:
        dipoles, charges, far_table, wide = refs
    else:
        copies, rows, table, far_table, wide = refs
    fields, potential = far_terms(far, far_table, wide, first_cell + core, own)
    for b in range(AB):
        pol = own[POL + b : POL + b + 1, :]
        for a in range(3):
            r = a * AB + b
            value = pol * (own[FIXED + r : FIXED + r + 1, :] + (near[r : r + 1, :] + fields[b][a]))
            if last:
                dipoles[a : a + 1, b * LANES : (b + 1) * LANES] = value
            else:
                rows[r : r + 1, :] = value
    for b in range(GB):
        value = own[BASE + b : BASE + b + 1, :] - own[RESP + b : RESP + b + 1, :] * (
            near[12 + b : 13 + b, :] + potential[b]
        )
        if last:
            charges[0:1, b * LANES : (b + 1) * LANES] = value
        else:
            rows[12 + b : 13 + b, :] = value
    if not last:
        share_sums(rows, own, table)
        everything = rows[...]
        for i in range(MEMBERS):
            copies[i] = everything


def swaps():
    pairs = []
    for c in range(1, CHIPS * CORES - 1, 2):
        for g in range(GROUPS):
            i, j = c * GROUPS + g, (c + 1) * GROUPS + g
            pairs += [(i, j), (j, i)]
    return pairs


def begin(sites, points, guess, fixed, pol, base, resp):
    return call(
        begin_kernel,
        (out(OWN, LANES), out(MEMBERS, FIRST, LANES)),
        (sites, points, guess, fixed, pol, base, resp),
        specs=[ANY] * 7,
        scratch=[
            pltpu.VMEM((FIRST, LANES), jnp.float32),
            pltpu.VMEM((8, LANES), jnp.float32),
            pltpu.VMEM((3, AB * LANES), jnp.float32),
            pltpu.VMEM((3, GB * LANES), jnp.float32),
            pltpu.VMEM((3, AB * LANES), jnp.float32),
            pltpu.VMEM((3, AB * LANES), jnp.float32),
            pltpu.SemaphoreType.DMA((4 + AB + 2 * GB,)),
        ],
        limit=60 << 20,
    )


def body(sites, points, guess, fixed, pol, base, resp, near, grids, sources):
    own, copies = begin(sites, points, guess, fixed, pol, base, resp)
    far_scratch = [
        pltpu.VMEM((CHIPS, LANES), jnp.float32),
        pltpu.VMEM((7 * VECTORS, 8, LANES), jnp.float32),
    ]
    static = static_halo = None
    for iteration in range(ITERS):
        last = iteration == ITERS - 1
        height = FIRST if iteration == 0 else DYN
        dyn = lax.all_to_all(copies, ("core", "grp"), 0, 0, tiled=True)
        static = dyn if static is None else static
        far_out, halo_out = call(
            sums_kernel, (out(CHIPS, 1, LANES), out(GROUPS, height, LANES)), (dyn,)
        )
        halo = lax.ppermute(halo_out, ("x", "z", "core", "grp"), swaps())
        far = lax.all_to_all(far_out, ("x", "z"), 0, 0, tiled=True)
        static_halo = halo if static_halo is None else static_halo
        near_field = call(
            near_kernel,
            out(16, LANES),
            (near, grids, sources, own, dyn, halo, static, static_halo),
            specs=[SM] * 3 + [VM] * 5,
            flops=40_000_000,
            scratch=[
                pltpu.VMEM((21, LANES, LANES), jnp.float32),
                pltpu.VMEM((15, LANES, LANES), jnp.float32),
                pltpu.VMEM((MEMBERS + GROUPS, DYN, LANES), jnp.float32),
                pltpu.VMEM((MEMBERS + GROUPS, FIRST - SITE, LANES), jnp.float32),
            ],
            limit=16 << 20,
        )
        if last:
            dipoles, charges = call(
                functools.partial(update_kernel, True),
                (out(3, AB * LANES), out(1, GB * LANES)),
                (own, near_field, far),
                scratch=far_scratch,
            )
        else:
            copies = call(
                functools.partial(update_kernel, False),
                out(MEMBERS, DYN, LANES),
                (own, near_field, far),
                scratch=[pltpu.VMEM((DYN, LANES), jnp.float32), pltpu.VMEM((8, LANES), jnp.float32)]
                + far_scratch,
            )
    return dipoles, charges.reshape(-1)


def solution(mesh):
    fine = Mesh(mesh.devices.reshape(X, Z, CORES, GROUPS), ("x", "z", "core", "grp"))
    every = ("x", "z", "core", "grp")
    return jax.shard_map(
        body,
        mesh=fine,
        in_specs=(P(None, every),) * 4 + (P(every),) * 3 + (P(every, None),) * 3,
        out_specs=(P(None, every), P(every)),
        check_vma=False,
    )
```

time: 121 us -> 112 us (0.926)
  Pallas kernels: 29.9 us -> 23.2 us
  waiting for transfers between devices: 3.13 us -> 7.84 us
  local copies, waits for them, and re-layouts: 4.16 us -> 0.02 us
  starting transfers between devices: 38.1 us -> 34.4 us
    pallas_call x10, Pallas kernels: 29.9 us -> 23.2 us  [call(): pl.pallas_call(kernel, out_shape=outs, in_specs=specs or [VM] * len(args)...]
    all_to_all x3, waiting for transfers between devices: 3.13 us -> 7.83 us  [body(): far = lax.all_to_all(far_out, ('x', 'z'), 0, 0, tiled=True)]
    all_to_all x3, starting transfers between devices: 27.2 us -> 24 us  [body(): far = lax.all_to_all(far_out, ('x', 'z'), 0, 0, tiled=True)]
    unnamed x16 -> x8, local copies, waits for them, and re-layouts: 2.79 us -> 0.02 us
    reshape x2 -> x0, local copies, waits for them, and re-layouts: 1.37 us -> none  [body(): flat = lambda v: v.reshape(1, -1)]
  transfers between devices with their start and end apart: 6 -> 6, of which waited for: 3 -> 3; matrix products, arithmetic and copies ran while one was open for 0% -> 0% of each run, Pallas kernels for 19% -> 16%
where the time goes in v2:
time: 112 us; the launch traced here: 111 us
  blocking collectives  44.3 us (40%)
  starting transfers between devices  34.4 us (31%)
  Pallas kernels  23.2 us (21%)
  waiting for transfers between devices  7.84 us (7%)
    all_to_all x3, blocking collectives, body(): dyn = lax.all_to_all(copies, ('core', 'grp'), 0, 0, tiled=True)  44.3 us
    all_to_all x3, starting transfers between devices, body(): far = lax.all_to_all(far_out, ('x', 'z'), 0, 0, tiled=True)  24 us
    pallas_call x10, Pallas kernels, call(): pl.pallas_call(kernel, out_shape=outs, in_specs=specs or [VM] * len(args)...  23.2 us
    ppermute x3, starting transfers between devices, body(): halo = lax.ppermute(halo_out, ('x', 'z', 'core', 'grp'), swaps())  10.3 us
    all_to_all x3, waiting for transfers between devices, body(): far = lax.all_to_all(far_out, ('x', 'z'), 0, 0, tiled=True)  7.83 us
  transfers between devices with their start and end apart: 6, of which 3 were waited for; matrix products, arithmetic and copies ran while one was open for 0% of the time, Pallas kernels for 16%

profile of v2, /device:TPU:1, one launch (start us, length us, event | category | flops | bytes accessed | tf_op | source)
XLA Modules:
  0.0 111.1 jit_solution(13105523174338921885)
XLA Ops:
  0.6 1.8 %shard_map.113 = (f32[48,128]{1,0:T(8,128)}, f32[16,40,128]{2,1,0:T(8,128)}) custom-call(f32[3,512]{1,0:T(4,128)} %sites.1, f32[3,384]{1,0:T(4,128)} %points.1, f32[3,512]{1,0:T(4,128)} %guess.1, f32[3,512]{1,0:T(4,128)} %fixed.1, f32[512]{0:T(512)} %pol.1, f32[384]{0:T(512)} %base.1, f32[384]{0:T(512)} %resp.1), custom_call_target="tpu_custom_call" | custom-call | flops 1000000 | bytes 1000 | tf_op jit(solution)/shard_map/pallas_call | solution.py:34
  2.4 21.0 %all_to_all.30.dyn.static = f32[16,40,128]{2,1,0:T(8,128)S(1)} all-to-all(f32[16,40,128]{2,1,0:T(8,128)} %get-tuple-element.13), channel_id=1, replica_groups=mesh['x'=4,'z'=8,'core'=2,'grp'=8] {'core','grp'}, dimensions={0} | all-to-all | bytes 655360 | tf_op jit(solution)/shard_map/all_to_all | solution.py:335
  23.4 0.6 shard_map.114
  24.0 0.0 copy-start
  24.0 3.6 %collective-permute-start = (f32[8,40,128]{2,1,0:T(8,128)S(1)}, f32[8,40,128]{2,1,0:T(8,128)S(1)}, u32[]{:S(2)}, u32[]{:S(2)}) collective-permute-start(f32[8,40,128]{2,1,0:T(8,128)S(1)} %get-tuple-element.14), channel_id=1, source_target_pairs={{8,16},{16,8},{9,17},{17,9},{10,18},{18,10},{11,19},{19,11},{12,20... | collective-permute-start | bytes 491528 | tf_op jit(solution)/shard_map/ppermute | solution.py:340
  27.6 0.0 copy-start.1
  27.6 0.0 copy-start.2
  27.6 0.0 copy-start.3
  27.6 12.1 %all-to-all-start.1 = ((f32[32,1,128]{2,1,0:T(1,128)}), f32[32,1,128]{2,1,0:T(1,128)S(1)}, u32[]{:S(2)}, u32[]{:S(2)}) async-start(f32[32,1,128]{2,1,0:T(1,128)} %get-tuple-element.15), calls=%async_computation.1 | async-start | bytes 32768 | tf_op jit(solution)/shard_map/all_to_all | solution.py:341
  39.8 0.0 collective-permute-done.dyn_halo.static_halo
  39.8 0.0 copy-done
  39.8 0.0 copy-done.1
  39.8 0.0 copy-done.2
  39.8 0.0 copy-done.3
  39.8 6.0 %shard_map.115.near = f32[16,128]{1,0:T(8,128)S(1)} custom-call(s32[4,8]{1,0:T(4,128)S(1)} %copy-done.1, s32[4,4]{1,0:T(4,128)S(1)} %copy-done.2, s32[3,8]{1,0:T(4,128)S(1)} %copy-done.3, f32[48,128]{1,0:T(8,128)S(1)} %copy-done, f32[16,40,128]{2,1,0:T(8,128)S(1)} %all_to_all.30.dyn.static, f32[8,40,128]{2,1,0:T(8,128)S(1)} %collective-permute-done.dyn_halo.static_halo, ...), custom_call_target="tpu_custom_call" | custom-call | flops 40000000 | bytes 1000 | tf_op jit(solution)/shard_map/pallas_call | solution.py:34
  45.8 2.6 %all-to-all-done.1.far = f32[32,1,128]{2,1,0:T(1,128)S(1)} async-done(((f32[32,1,128]{2,1,0:T(1,128)}), f32[32,1,128]{2,1,0:T(1,128)S(1)}, u32[]{:S(2)}, u32[]{:S(2)}) %all-to-all-start.1) | async-done | bytes 16416 | tf_op jit(solution)/shard_map/all_to_all | solution.py:341
  48.4 0.4 shard_map.116
  48.8 11.8 %all_to_all.31.dyn = f32[16,16,128]{2,1,0:T(8,128)S(1)} all-to-all(f32[16,16,128]{2,1,0:T(8,128)S(1)} %shard_map.116), channel_id=1, replica_groups=mesh['x'=4,'z'=8,'core'=2,'grp'=8] {'core','grp'}, dimensions={0} | all-to-all | bytes 262144 | tf_op jit(solution)/shard_map/all_to_all | solution.py:335
  60.6 0.6 shard_map.117
  61.2 3.4 %collective-permute-start.1 = (f32[8,16,128]{2,1,0:T(8,128)S(1)}, f32[8,16,128]{2,1,0:T(8,128)S(1)}, u32[]{:S(2)}, u32[]{:S(2)}) collective-permute-start(f32[8,16,128]{2,1,0:T(8,128)S(1)} %get-tuple-element.16), channel_id=1, source_target_pairs={{8,16},{16,8},{9,17},{17,9},{10,18},{18,10},{11,19},{19,11},{12,20... | collective-permute-start | bytes 196616 | tf_op jit(solution)/shard_map/ppermute | solution.py:340
  64.5 6.2 %all-to-all-start.3 = ((f32[32,1,128]{2,1,0:T(1,128)}), f32[32,1,128]{2,1,0:T(1,128)S(1)}, u32[]{:S(2)}, u32[]{:S(2)}) async-start(f32[32,1,128]{2,1,0:T(1,128)} %get-tuple-element.17), calls=%async_computation.3 | async-start | bytes 32768 | tf_op jit(solution)/shard_map/all_to_all | solution.py:341
  70.7 0.0 collective-permute-done.1.dyn_halo
  70.8 6.0 %shard_map.118.near = f32[16,128]{1,0:T(8,128)S(1)} custom-call(s32[4,8]{1,0:T(4,128)S(1)} %copy-done.1, s32[4,4]{1,0:T(4,128)S(1)} %copy-done.2, s32[3,8]{1,0:T(4,128)S(1)} %copy-done.3, f32[48,128]{1,0:T(8,128)S(1)} %copy-done, f32[16,16,128]{2,1,0:T(8,128)S(1)} %all_to_all.31.dyn, f32[8,16,128]{2,1,0:T(8,128)S(1)} %collective-permute-done.1.dyn_halo, ...), custom_call_target="tpu_custom_call" | custom-call | flops 40000000 | bytes 1000 | tf_op jit(solution)/shard_map/pallas_call | solution.py:34
  76.8 2.6 %all-to-all-done.3.far = f32[32,1,128]{2,1,0:T(1,128)S(1)} async-done(((f32[32,1,128]{2,1,0:T(1,128)}), f32[32,1,128]{2,1,0:T(1,128)S(1)}, u32[]{:S(2)}, u32[]{:S(2)}) %all-to-all-start.3) | async-done | bytes 16416 | tf_op jit(solution)/shard_map/all_to_all | solution.py:341
  79.4 0.4 shard_map.119
  79.8 11.6 %all_to_all.32.dyn = f32[16,16,128]{2,1,0:T(8,128)S(1)} all-to-all(f32[16,16,128]{2,1,0:T(8,128)S(1)} %shard_map.119), channel_id=1, replica_groups=mesh['x'=4,'z'=8,'core'=2,'grp'=8] {'core','grp'}, dimensions={0} | all-to-all | bytes 262144 | tf_op jit(solution)/shard_map/all_to_all | solution.py:335
  91.3 0.6 shard_map.120
  91.9 3.4 %collective-permute-start.2 = (f32[8,16,128]{2,1,0:T(8,128)S(1)}, f32[8,16,128]{2,1,0:T(8,128)S(1)}, u32[]{:S(2)}, u32[]{:S(2)}) collective-permute-start(f32[8,16,128]{2,1,0:T(8,128)S(1)} %get-tuple-element.18), channel_id=1, source_target_pairs={{8,16},{16,8},{9,17},{17,9},{10,18},{18,10},{11,19},{19,11},{12,20... | collective-permute-start | bytes 196616 | tf_op jit(solution)/shard_map/ppermute | solution.py:340
  95.3 5.7 %all-to-all-start.5 = ((f32[32,1,128]{2,1,0:T(1,128)}), f32[32,1,128]{2,1,0:T(1,128)S(1)}, u32[]{:S(2)}, u32[]{:S(2)}) async-start(f32[32,1,128]{2,1,0:T(1,128)} %get-tuple-element.19), calls=%async_computation.5 | async-start | bytes 32768 | tf_op jit(solution)/shard_map/all_to_all | solution.py:341
  101.0 0.0 collective-permute-done.2.dyn_halo
  101.1 6.0 %shard_map.121.near = f32[16,128]{1,0:T(8,128)S(1)} custom-call(s32[4,8]{1,0:T(4,128)S(1)} %copy-done.1, s32[4,4]{1,0:T(4,128)S(1)} %copy-done.2, s32[3,8]{1,0:T(4,128)S(1)} %copy-done.3, f32[48,128]{1,0:T(8,128)S(1)} %copy-done, f32[16,16,128]{2,1,0:T(8,128)S(1)} %all_to_all.32.dyn, f32[8,16,128]{2,1,0:T(8,128)S(1)} %collective-permute-done.2.dyn_halo, ...), custom_call_target="tpu_custom_call" | custom-call | flops 40000000 | bytes 1000 | tf_op jit(solution)/shard_map/pallas_call | solution.py:34
  107.1 2.6 %all-to-all-done.5.far = f32[32,1,128]{2,1,0:T(1,128)S(1)} async-done(((f32[32,1,128]{2,1,0:T(1,128)}), f32[32,1,128]{2,1,0:T(1,128)S(1)}, u32[]{:S(2)}, u32[]{:S(2)}) %all-to-all-start.5) | async-done | bytes 16416 | tf_op jit(solution)/shard_map/all_to_all | solution.py:341
  109.7 0.8 shard_map.122
  110.5 0.6 reduce
Async XLA Ops:
  24.0 15.8 %copy-start = (f32[48,128]{1,0:T(8,128)S(1)}, f32[48,128]{1,0:T(8,128)}, u32[]{:S(2)}) copy-start(f32[48,128]{1,0:T(8,128)} %get-tuple-element.12.own) | copy-start | bytes 73732
  24.0 15.8 %collective-permute-start = (f32[8,40,128]{2,1,0:T(8,128)S(1)}, f32[8,40,128]{2,1,0:T(8,128)S(1)}, u32[]{:S(2)}, u32[]{:S(2)}) collective-permute-start(f32[8,40,128]{2,1,0:T(8,128)S(1)} %get-tuple-element.14), channel_id=1, source_target_pairs={{8,16},{16,8},{9,17},{17,9},{10,18},{18,10},{11,19},{19,11},{12,20... | collective-permute-start | bytes 491528 | tf_op jit(solution)/shard_map/ppermute | solution.py:340
  27.6 12.2 %copy-start.1 = (s32[4,8]{1,0:T(4,128)S(1)}, s32[4,8]{1,0:T(4,128)}, u32[]{:S(2)}) copy-start(s32[4,8]{1,0:T(4,128)} %near.5) | copy-start | bytes 388
  27.6 12.2 %copy-start.2 = (s32[4,4]{1,0:T(4,128)S(1)}, s32[4,4]{1,0:T(4,128)}, u32[]{:S(2)}) copy-start(s32[4,4]{1,0:T(4,128)} %grids.5) | copy-start | bytes 196
  27.6 12.2 %copy-start.3 = (s32[3,8]{1,0:T(4,128)S(1)}, s32[3,8]{1,0:T(4,128)}, u32[]{:S(2)}) copy-start(s32[3,8]{1,0:T(4,128)} %sources.5) | copy-start | bytes 292
  27.6 20.8 %all-to-all-start.1 = ((f32[32,1,128]{2,1,0:T(1,128)}), f32[32,1,128]{2,1,0:T(1,128)S(1)}, u32[]{:S(2)}, u32[]{:S(2)}) async-start(f32[32,1,128]{2,1,0:T(1,128)} %get-tuple-element.15), calls=%async_computation.1 | async-start | bytes 32768 | tf_op jit(solution)/shard_map/all_to_all | solution.py:341
  61.2 9.6 %collective-permute-start.1 = (f32[8,16,128]{2,1,0:T(8,128)S(1)}, f32[8,16,128]{2,1,0:T(8,128)S(1)}, u32[]{:S(2)}, u32[]{:S(2)}) collective-permute-start(f32[8,16,128]{2,1,0:T(8,128)S(1)} %get-tuple-element.16), channel_id=1, source_target_pairs={{8,16},{16,8},{9,17},{17,9},{10,18},{18,10},{11,19},{19,11},{12,20... | collective-permute-start | bytes 196616 | tf_op jit(solution)/shard_map/ppermute | solution.py:340
  64.5 14.9 %all-to-all-start.3 = ((f32[32,1,128]{2,1,0:T(1,128)}), f32[32,1,128]{2,1,0:T(1,128)S(1)}, u32[]{:S(2)}, u32[]{:S(2)}) async-start(f32[32,1,128]{2,1,0:T(1,128)} %get-tuple-element.17), calls=%async_computation.3 | async-start | bytes 32768 | tf_op jit(solution)/shard_map/all_to_all | solution.py:341
  91.9 9.1 %collective-permute-start.2 = (f32[8,16,128]{2,1,0:T(8,128)S(1)}, f32[8,16,128]{2,1,0:T(8,128)S(1)}, u32[]{:S(2)}, u32[]{:S(2)}) collective-permute-start(f32[8,16,128]{2,1,0:T(8,128)S(1)} %get-tuple-element.18), channel_id=1, source_target_pairs={{8,16},{16,8},{9,17},{17,9},{10,18},{18,10},{11,19},{19,11},{12,20... | collective-permute-start | bytes 196616 | tf_op jit(solution)/shard_map/ppermute | solution.py:340
  95.3 14.4 %all-to-all-start.5 = ((f32[32,1,128]{2,1,0:T(1,128)}), f32[32,1,128]{2,1,0:T(1,128)S(1)}, u32[]{:S(2)}, u32[]{:S(2)}) async-start(f32[32,1,128]{2,1,0:T(1,128)} %get-tuple-element.19), calls=%async_computation.5 | async-start | bytes 32768 | tf_op jit(solution)/shard_map/all_to_all | solution.py:341

commit v3 on v2

--- a/solution.py
+++ b/solution.py
@@ -163,9 +163,12 @@
 
     me = second + lax.axis_index("grp")
 
+    def finished(r):
+        result[r : r + 1, :] = jnp.sum(jnp.transpose(sums[r]), axis=0, keepdims=True)
+
     def atom_chunk(step, carry):
         tb = step // (LANES // CHUNK)
-        start = pl.multiple_of((step - tb * (LANES // CHUNK)) * CHUNK, CHUNK)
+        start = 0
         t = [columns[a * AB + tb, pl.ds(start, CHUNK), :] for a in range(3)]
         acc = [jnp.zeros((CHUNK, LANES), jnp.float32) for _ in range(3)]
         for n in range(9):
@@ -196,7 +199,7 @@
 
     def grid_chunk(step, carry):
         tb = step // (LANES // CHUNK)
-        start = pl.multiple_of((step - tb * (LANES // CHUNK)) * CHUNK, CHUNK)
+        start = 0
         t = [columns[12 + a * GB + tb, pl.ds(start, CHUNK), :] for a in range(3)]
         acc = jnp.zeros((CHUNK, LANES), jnp.float32)
         for n in range(8):
@@ -208,10 +211,13 @@
         sums[12 + tb, pl.ds(start, CHUNK), :] = acc
         return carry
 
-    lax.fori_loop(0, AB * (LANES // CHUNK), atom_chunk, 0)
-    lax.fori_loop(0, GB * (LANES // CHUNK), grid_chunk, 0)
-    for r in range(12 + GB):
-        result[r : r + 1, :] = jnp.sum(jnp.transpose(sums[r]), axis=0, keepdims=True)
+    for step in range(AB):
+        atom_chunk(step, 0)
+        for a in range(3):
+            finished(a * AB + step)
+    for step in range(GB):
+        grid_chunk(step, 0)
+        finished(12 + step)
     result[15:16, :] = jnp.zeros((1, LANES), jnp.float32)
 
 
@@ -284,7 +290,7 @@
             near[12 + b : 13 + b, :] + potential[b]
         )
         if last:
-            charges[0:1, b * LANES : (b + 1) * LANES] = value
+            charges[b * LANES : (b + 1) * LANES] = value[0]
         else:
             rows[12 + b : 13 + b, :] = value
     if not last:
@@ -357,7 +363,7 @@
         if last:
             dipoles, charges = call(
                 functools.partial(update_kernel, True),
-                (out(3, AB * LANES), out(1, GB * LANES)),
+                (out(3, AB * LANES), out(GB * LANES)),
                 (own, near_field, far),
                 scratch=far_scratch,
             )
@@ -369,7 +375,7 @@
                 scratch=[pltpu.VMEM((DYN, LANES), jnp.float32), pltpu.VMEM((8, LANES), jnp.float32)]
                 + far_scratch,
             )
-    return dipoles, charges.reshape(-1)
+    return dipoles, charges
 
 
 def solution(mesh):

time: 112 us -> 110 us (0.982)
  Pallas kernels: 23.2 us -> 21.3 us
  waiting for transfers between devices: 7.84 us -> 9.66 us
    pallas_call x10, Pallas kernels: 23.2 us -> 21.3 us  [call(): pl.pallas_call(kernel, out_shape=outs, in_specs=specs or [VM] * len(args)...]
    all_to_all x3, waiting for transfers between devices: 7.83 us -> 9.65 us  [body(): far = lax.all_to_all(far_out, ('x', 'z'), 0, 0, tiled=True)]
  transfers between devices with their start and end apart: 6 -> 6, of which waited for: 3 -> 3; matrix products, arithmetic and copies ran while one was open for 0% -> 0% of each run, Pallas kernels for 16% -> 15%
where the time goes in v3:
time: 110 us
  blocking collectives  44.3 us (40%)
  starting transfers between devices  33.8 us (31%)
  Pallas kernels  21.3 us (19%)
  waiting for transfers between devices  9.66 us (9%)
    all_to_all x3, blocking collectives, body(): dyn = lax.all_to_all(copies, ('core', 'grp'), 0, 0, tiled=True)  44.3 us
    all_to_all x3, starting transfers between devices, body(): far = lax.all_to_all(far_out, ('x', 'z'), 0, 0, tiled=True)  23.4 us
    pallas_call x10, Pallas kernels, call(): pl.pallas_call(kernel, out_shape=outs, in_specs=specs or [VM] * len(args)...  21.3 us
    ppermute x3, starting transfers between devices, body(): halo = lax.ppermute(halo_out, ('x', 'z', 'core', 'grp'), swaps())  10.4 us
    all_to_all x3, waiting for transfers between devices, body(): far = lax.all_to_all(far_out, ('x', 'z'), 0, 0, tiled=True)  9.65 us
  transfers between devices with their start and end apart: 6, of which 3 were waited for; matrix products, arithmetic and copies ran while one was open for 0% of the time, Pallas kernels for 15%

profile of v3, /device:TPU:1, one launch (start us, length us, event | category | flops | bytes accessed | tf_op | source)
XLA Modules:
  0.0 109.8 jit_solution(10630837639107555434)
XLA Ops:
  0.6 1.8 %shard_map.113 = (f32[48,128]{1,0:T(8,128)}, f32[16,40,128]{2,1,0:T(8,128)}) custom-call(f32[3,512]{1,0:T(4,128)} %sites.1, f32[3,384]{1,0:T(4,128)} %points.1, f32[3,512]{1,0:T(4,128)} %guess.1, f32[3,512]{1,0:T(4,128)} %fixed.1, f32[512]{0:T(512)} %pol.1, f32[384]{0:T(512)} %base.1, f32[384]{0:T(512)} %resp.1), custom_call_target="tpu_custom_call" | custom-call | flops 1000000 | bytes 1000 | tf_op jit(solution)/shard_map/pallas_call | solution.py:34
  2.4 21.0 %all_to_all.30.dyn.static = f32[16,40,128]{2,1,0:T(8,128)S(1)} all-to-all(f32[16,40,128]{2,1,0:T(8,128)} %get-tuple-element.11), channel_id=1, replica_groups=mesh['x'=4,'z'=8,'core'=2,'grp'=8] {'core','grp'}, dimensions={0} | all-to-all | bytes 655360 | tf_op jit(solution)/shard_map/all_to_all | solution.py:341
  23.4 0.6 shard_map.114
  24.0 0.0 copy-start
  24.0 3.6 %collective-permute-start = (f32[8,40,128]{2,1,0:T(8,128)S(1)}, f32[8,40,128]{2,1,0:T(8,128)S(1)}, u32[]{:S(2)}, u32[]{:S(2)}) collective-permute-start(f32[8,40,128]{2,1,0:T(8,128)S(1)} %get-tuple-element.12), channel_id=1, source_target_pairs={{8,16},{16,8},{9,17},{17,9},{10,18},{18,10},{11,19},{19,11},{12,20... | collective-permute-start | bytes 491528 | tf_op jit(solution)/shard_map/ppermute | solution.py:346
  27.6 0.0 copy-start.1
  27.6 0.0 copy-start.2
  27.6 0.0 copy-start.3
  27.7 12.1 %all-to-all-start.1 = ((f32[32,1,128]{2,1,0:T(1,128)}), f32[32,1,128]{2,1,0:T(1,128)S(1)}, u32[]{:S(2)}, u32[]{:S(2)}) async-start(f32[32,1,128]{2,1,0:T(1,128)} %get-tuple-element.13), calls=%async_computation.1 | async-start | bytes 32768 | tf_op jit(solution)/shard_map/all_to_all | solution.py:347
  39.8 0.0 collective-permute-done.dyn_halo.static_halo
  39.8 0.0 copy-done
  39.8 0.0 copy-done.1
  39.8 0.0 copy-done.2
  39.8 0.0 copy-done.3
  39.8 5.4 %shard_map.115.near = f32[16,128]{1,0:T(8,128)S(1)} custom-call(s32[4,8]{1,0:T(4,128)S(1)} %copy-done.1, s32[4,4]{1,0:T(4,128)S(1)} %copy-done.2, s32[3,8]{1,0:T(4,128)S(1)} %copy-done.3, f32[48,128]{1,0:T(8,128)S(1)} %copy-done, f32[16,40,128]{2,1,0:T(8,128)S(1)} %all_to_all.30.dyn.static, f32[8,40,128]{2,1,0:T(8,128)S(1)} %collective-permute-done.dyn_halo.static_halo, ...), custom_call_target="tpu_custom_call" | custom-call | flops 40000000 | bytes 1000 | tf_op jit(solution)/shard_map/pallas_call | solution.py:34
  45.2 3.2 %all-to-all-done.1.far = f32[32,1,128]{2,1,0:T(1,128)S(1)} async-done(((f32[32,1,128]{2,1,0:T(1,128)}), f32[32,1,128]{2,1,0:T(1,128)S(1)}, u32[]{:S(2)}, u32[]{:S(2)}) %all-to-all-start.1) | async-done | bytes 16416 | tf_op jit(solution)/shard_map/all_to_all | solution.py:347
  48.4 0.4 shard_map.116
  48.8 11.8 %all_to_all.31.dyn = f32[16,16,128]{2,1,0:T(8,128)S(1)} all-to-all(f32[16,16,128]{2,1,0:T(8,128)S(1)} %shard_map.116), channel_id=1, replica_groups=mesh['x'=4,'z'=8,'core'=2,'grp'=8] {'core','grp'}, dimensions={0} | all-to-all | bytes 262144 | tf_op jit(solution)/shard_map/all_to_all | solution.py:341
  60.5 0.6 shard_map.117
  61.1 3.4 %collective-permute-start.1 = (f32[8,16,128]{2,1,0:T(8,128)S(1)}, f32[8,16,128]{2,1,0:T(8,128)S(1)}, u32[]{:S(2)}, u32[]{:S(2)}) collective-permute-start(f32[8,16,128]{2,1,0:T(8,128)S(1)} %get-tuple-element.14), channel_id=1, source_target_pairs={{8,16},{16,8},{9,17},{17,9},{10,18},{18,10},{11,19},{19,11},{12,20... | collective-permute-start | bytes 196616 | tf_op jit(solution)/shard_map/ppermute | solution.py:346
  64.5 5.8 %all-to-all-start.3 = ((f32[32,1,128]{2,1,0:T(1,128)}), f32[32,1,128]{2,1,0:T(1,128)S(1)}, u32[]{:S(2)}, u32[]{:S(2)}) async-start(f32[32,1,128]{2,1,0:T(1,128)} %get-tuple-element.15), calls=%async_computation.3 | async-start | bytes 32768 | tf_op jit(solution)/shard_map/all_to_all | solution.py:347
  70.3 0.0 collective-permute-done.1.dyn_halo
  70.3 5.4 %shard_map.118.near = f32[16,128]{1,0:T(8,128)S(1)} custom-call(s32[4,8]{1,0:T(4,128)S(1)} %copy-done.1, s32[4,4]{1,0:T(4,128)S(1)} %copy-done.2, s32[3,8]{1,0:T(4,128)S(1)} %copy-done.3, f32[48,128]{1,0:T(8,128)S(1)} %copy-done, f32[16,16,128]{2,1,0:T(8,128)S(1)} %all_to_all.31.dyn, f32[8,16,128]{2,1,0:T(8,128)S(1)} %collective-permute-done.1.dyn_halo, ...), custom_call_target="tpu_custom_call" | custom-call | flops 40000000 | bytes 1000 | tf_op jit(solution)/shard_map/pallas_call | solution.py:34
  75.7 3.1 %all-to-all-done.3.far = f32[32,1,128]{2,1,0:T(1,128)S(1)} async-done(((f32[32,1,128]{2,1,0:T(1,128)}), f32[32,1,128]{2,1,0:T(1,128)S(1)}, u32[]{:S(2)}, u32[]{:S(2)}) %all-to-all-start.3) | async-done | bytes 16416 | tf_op jit(solution)/shard_map/all_to_all | solution.py:347
  78.8 0.4 shard_map.119
  79.1 11.6 %all_to_all.32.dyn = f32[16,16,128]{2,1,0:T(8,128)S(1)} all-to-all(f32[16,16,128]{2,1,0:T(8,128)S(1)} %shard_map.119), channel_id=1, replica_groups=mesh['x'=4,'z'=8,'core'=2,'grp'=8] {'core','grp'}, dimensions={0} | all-to-all | bytes 262144 | tf_op jit(solution)/shard_map/all_to_all | solution.py:341
  90.7 0.6 shard_map.120
  91.3 3.4 %collective-permute-start.2 = (f32[8,16,128]{2,1,0:T(8,128)S(1)}, f32[8,16,128]{2,1,0:T(8,128)S(1)}, u32[]{:S(2)}, u32[]{:S(2)}) collective-permute-start(f32[8,16,128]{2,1,0:T(8,128)S(1)} %get-tuple-element.16), channel_id=1, source_target_pairs={{8,16},{16,8},{9,17},{17,9},{10,18},{18,10},{11,19},{19,11},{12,20... | collective-permute-start | bytes 196616 | tf_op jit(solution)/shard_map/ppermute | solution.py:346
  94.7 5.5 %all-to-all-start.5 = ((f32[32,1,128]{2,1,0:T(1,128)}), f32[32,1,128]{2,1,0:T(1,128)S(1)}, u32[]{:S(2)}, u32[]{:S(2)}) async-start(f32[32,1,128]{2,1,0:T(1,128)} %get-tuple-element.17), calls=%async_computation.5 | async-start | bytes 32768 | tf_op jit(solution)/shard_map/all_to_all | solution.py:347
  100.2 0.0 collective-permute-done.2.dyn_halo
  100.3 5.4 %shard_map.121.near = f32[16,128]{1,0:T(8,128)S(1)} custom-call(s32[4,8]{1,0:T(4,128)S(1)} %copy-done.1, s32[4,4]{1,0:T(4,128)S(1)} %copy-done.2, s32[3,8]{1,0:T(4,128)S(1)} %copy-done.3, f32[48,128]{1,0:T(8,128)S(1)} %copy-done, f32[16,16,128]{2,1,0:T(8,128)S(1)} %all_to_all.32.dyn, f32[8,16,128]{2,1,0:T(8,128)S(1)} %collective-permute-done.2.dyn_halo, ...), custom_call_target="tpu_custom_call" | custom-call | flops 40000000 | bytes 1000 | tf_op jit(solution)/shard_map/pallas_call | solution.py:34
  105.6 3.3 %all-to-all-done.5.far = f32[32,1,128]{2,1,0:T(1,128)S(1)} async-done(((f32[32,1,128]{2,1,0:T(1,128)}), f32[32,1,128]{2,1,0:T(1,128)S(1)}, u32[]{:S(2)}, u32[]{:S(2)}) %all-to-all-start.5) | async-done | bytes 16416 | tf_op jit(solution)/shard_map/all_to_all | solution.py:347
  108.9 0.8 shard_map.122
Async XLA Ops:
  24.0 15.8 %copy-start = (f32[48,128]{1,0:T(8,128)S(1)}, f32[48,128]{1,0:T(8,128)}, u32[]{:S(2)}) copy-start(f32[48,128]{1,0:T(8,128)} %get-tuple-element.10.own) | copy-start | bytes 73732
  24.0 15.8 %collective-permute-start = (f32[8,40,128]{2,1,0:T(8,128)S(1)}, f32[8,40,128]{2,1,0:T(8,128)S(1)}, u32[]{:S(2)}, u32[]{:S(2)}) collective-permute-start(f32[8,40,128]{2,1,0:T(8,128)S(1)} %get-tuple-element.12), channel_id=1, source_target_pairs={{8,16},{16,8},{9,17},{17,9},{10,18},{18,10},{11,19},{19,11},{12,20... | collective-permute-start | bytes 491528 | tf_op jit(solution)/shard_map/ppermute | solution.py:346
  27.6 12.2 %copy-start.1 = (s32[4,8]{1,0:T(4,128)S(1)}, s32[4,8]{1,0:T(4,128)}, u32[]{:S(2)}) copy-start(s32[4,8]{1,0:T(4,128)} %near.5) | copy-start | bytes 388
  27.6 12.2 %copy-start.2 = (s32[4,4]{1,0:T(4,128)S(1)}, s32[4,4]{1,0:T(4,128)}, u32[]{:S(2)}) copy-start(s32[4,4]{1,0:T(4,128)} %grids.5) | copy-start | bytes 196
  27.6 12.2 %copy-start.3 = (s32[3,8]{1,0:T(4,128)S(1)}, s32[3,8]{1,0:T(4,128)}, u32[]{:S(2)}) copy-start(s32[3,8]{1,0:T(4,128)} %sources.5) | copy-start | bytes 292
  27.7 20.8 %all-to-all-start.1 = ((f32[32,1,128]{2,1,0:T(1,128)}), f32[32,1,128]{2,1,0:T(1,128)S(1)}, u32[]{:S(2)}, u32[]{:S(2)}) async-start(f32[32,1,128]{2,1,0:T(1,128)} %get-tuple-element.13), calls=%async_computation.1 | async-start | bytes 32768 | tf_op jit(solution)/shard_map/all_to_all | solution.py:347
  61.1 9.2 %collective-permute-start.1 = (f32[8,16,128]{2,1,0:T(8,128)S(1)}, f32[8,16,128]{2,1,0:T(8,128)S(1)}, u32[]{:S(2)}, u32[]{:S(2)}) collective-permute-start(f32[8,16,128]{2,1,0:T(8,128)S(1)} %get-tuple-element.14), channel_id=1, source_target_pairs={{8,16},{16,8},{9,17},{17,9},{10,18},{18,10},{11,19},{19,11},{12,20... | collective-permute-start | bytes 196616 | tf_op jit(solution)/shard_map/ppermute | solution.py:346
  64.5 14.2 %all-to-all-start.3 = ((f32[32,1,128]{2,1,0:T(1,128)}), f32[32,1,128]{2,1,0:T(1,128)S(1)}, u32[]{:S(2)}, u32[]{:S(2)}) async-start(f32[32,1,128]{2,1,0:T(1,128)} %get-tuple-element.15), calls=%async_computation.3 | async-start | bytes 32768 | tf_op jit(solution)/shard_map/all_to_all | solution.py:347
  91.3 8.9 %collective-permute-start.2 = (f32[8,16,128]{2,1,0:T(8,128)S(1)}, f32[8,16,128]{2,1,0:T(8,128)S(1)}, u32[]{:S(2)}, u32[]{:S(2)}) collective-permute-start(f32[8,16,128]{2,1,0:T(8,128)S(1)} %get-tuple-element.16), channel_id=1, source_target_pairs={{8,16},{16,8},{9,17},{17,9},{10,18},{18,10},{11,19},{19,11},{12,20... | collective-permute-start | bytes 196616 | tf_op jit(solution)/shard_map/ppermute | solution.py:346
  94.7 14.2 %all-to-all-start.5 = ((f32[32,1,128]{2,1,0:T(1,128)}), f32[32,1,128]{2,1,0:T(1,128)S(1)}, u32[]{:S(2)}, u32[]{:S(2)}) async-start(f32[32,1,128]{2,1,0:T(1,128)} %get-tuple-element.17), calls=%async_computation.5 | async-start | bytes 32768 | tf_op jit(solution)/shard_map/all_to_all | solution.py:347

commit v4 on v3

--- a/solution.py
+++ b/solution.py
@@ -107,15 +107,16 @@
     core, _ = position()
     totals = []
     for k in range(CORES):
-        total = dyn[k * GROUPS, 15:16, :]
-        for g in range(1, GROUPS):
-            total = total + dyn[k * GROUPS + g, 15:16, :]
+        total = None
+        for g in range(GROUPS):
+            part = dyn[MEMBERS - 1 - k * GROUPS - g, 15:16, :]
+            total = part if total is None else total + part
         totals.append(total)
     lane = lax.broadcasted_iota(jnp.int32, (1, LANES), 1)
     row = jnp.where(lane < 8, totals[0], totals[1])
     for i in range(CHIPS):
         far[i] = row
-    halo[...] = dyn[pl.ds(core * GROUPS, GROUPS)]
+    halo[...] = dyn[pl.ds((CORES - 1 - core) * GROUPS, GROUPS)]
 
 
 def geometry(t, s):
@@ -132,10 +133,12 @@
     near, grids, sources, own, dyn, dyn_halo, static, static_halo, result, columns, sums, moving, fixed
 ):
     core, _ = position()
-    moving[0:MEMBERS] = dyn[:, 0:DYN, :]
-    moving[MEMBERS:] = dyn_halo[:, 0:DYN, :]
-    fixed[0:MEMBERS] = static[:, SITE:FIRST, :]
-    fixed[MEMBERS:] = static_halo[:, SITE:FIRST, :]
+    for m in range(MEMBERS):
+        moving[m] = dyn[MEMBERS - 1 - m, 0:DYN, :]
+        fixed[m] = static[MEMBERS - 1 - m, SITE:FIRST, :]
+    for g in range(GROUPS):
+        moving[MEMBERS + g] = dyn_halo[GROUPS - 1 - g, 0:DYN, :]
+        fixed[MEMBERS + g] = static_halo[GROUPS - 1 - g, SITE:FIRST, :]
     for r in range(3 * AB + 3 * GB):
         columns[r] = jnp.transpose(jnp.broadcast_to(own[r : r + 1, :], (LANES, LANES)))
 
@@ -226,7 +229,7 @@
 
 def far_terms(far, table, wide, here, own):
     for i in range(CHIPS):
-        table[i : i + 1, :] = far[i]
+        table[i : i + 1, :] = far[CHIPS - 1 - i]
     centres, masks = [], []
     for n in range(VECTORS):
         k, v = n // (CHIPS // 8), n % (CHIPS // 8)
@@ -300,6 +303,14 @@
             copies[i] = everything
 
 
+def columns():
+    return [[chip * MEMBERS + m for m in reversed(range(MEMBERS))] for chip in range(CHIPS)]
+
+
+def planes():
+    return [[chip * MEMBERS + m for chip in reversed(range(CHIPS))] for m in range(MEMBERS)]
+
+
 def swaps():
     pairs = []
     for c in range(1, CHIPS * CORES - 1, 2):
@@ -335,16 +346,17 @@
         pltpu.VMEM((7 * VECTORS, 8, LANES), jnp.float32),
     ]
     static = static_halo = None
+    every = ("x", "z", "core", "grp")
     for iteration in range(ITERS):
         last = iteration == ITERS - 1
         height = FIRST if iteration == 0 else DYN
-        dyn = lax.all_to_all(copies, ("core", "grp"), 0, 0, tiled=True)
+        dyn = lax.all_to_all(copies, every, 0, 0, axis_index_groups=columns(), tiled=True)
         static = dyn if static is None else static
         far_out, halo_out = call(
             sums_kernel, (out(CHIPS, 1, LANES), out(GROUPS, height, LANES)), (dyn,)
         )
-        halo = lax.ppermute(halo_out, ("x", "z", "core", "grp"), swaps())
-        far = lax.all_to_all(far_out, ("x", "z"), 0, 0, tiled=True)
+        halo = lax.ppermute(halo_out, every, swaps())
+        far = lax.all_to_all(far_out, every, 0, 0, axis_index_groups=planes(), tiled=True)
         static_halo = halo if static_halo is None else static_halo
         near_field = call(
             near_kernel,

time: 110 us -> 107 us (0.973)
  waiting for transfers between devices: 9.66 us -> 0.02 us
  starting transfers between devices: 33.8 us -> 38.1 us
  blocking collectives: 44.3 us -> 46.3 us
    all_to_all x3, waiting for transfers between devices: 9.65 us -> 0.01 us  [body(): lax.all_to_all(far_out, every, 0, 0, axis_index_groups=planes(), tiled=True)]
    all_to_all x3, starting transfers between devices: 23.4 us -> 30 us  [body(): lax.all_to_all(far_out, every, 0, 0, axis_index_groups=planes(), tiled=True)]
    ppermute x3, starting transfers between devices: 10.4 us -> 8.06 us  [body(): halo = lax.ppermute(halo_out, every, swaps())]
    all_to_all x3, blocking collectives: 44.3 us -> 46.3 us  [body(): lax.all_to_all(copies, every, 0, 0, axis_index_groups=columns(), tiled=True)]
  transfers between devices with their start and end apart: 6 -> 6, of which waited for: 3 -> 0; matrix products, arithmetic and copies ran while one was open for 0% -> 0% of each run, Pallas kernels for 15% -> 15%
where the time goes in v4:
time: 107 us; the launch traced here: 106 us
  blocking collectives  46.3 us (43%)
  starting transfers between devices  38.1 us (36%)
  Pallas kernels  21.3 us (20%)
    all_to_all x3, blocking collectives, body(): lax.all_to_all(copies, every, 0, 0, axis_index_groups=columns(), tiled=True)  46.3 us
    all_to_all x3, starting transfers between devices, body(): lax.all_to_all(far_out, every, 0, 0, axis_index_groups=planes(), tiled=True)  30 us
    pallas_call x10, Pallas kernels, call(): pl.pallas_call(kernel, out_shape=outs, in_specs=specs or [VM] * len(args)...  21.3 us
    ppermute x3, starting transfers between devices, body(): halo = lax.ppermute(halo_out, every, swaps())  8.06 us
  transfers between devices with their start and end apart: 6, of which 0 were waited for; matrix products, arithmetic and copies ran while one was open for 0% of the time, Pallas kernels for 15%

profile of v4, /device:TPU:1, one launch (start us, length us, event | category | flops | bytes accessed | tf_op | source)
XLA Modules:
  0.0 106.5 jit_solution(14689239674283038912)
XLA Ops:
  0.6 1.8 %shard_map.113 = (f32[48,128]{1,0:T(8,128)}, f32[16,40,128]{2,1,0:T(8,128)}) custom-call(f32[3,512]{1,0:T(4,128)} %sites.1, f32[3,384]{1,0:T(4,128)} %points.1, f32[3,512]{1,0:T(4,128)} %guess.1, f32[3,512]{1,0:T(4,128)} %fixed.1, f32[512]{0:T(512)} %pol.1, f32[384]{0:T(512)} %base.1, f32[384]{0:T(512)} %resp.1), custom_call_target="tpu_custom_call" | custom-call | flops 1000000 | bytes 1000 | tf_op jit(solution)/shard_map/pallas_call | solution.py:34
  2.4 21.6 %all_to_all.30.dyn.static = f32[16,40,128]{2,1,0:T(8,128)S(1)} all-to-all(f32[16,40,128]{2,1,0:T(8,128)} %get-tuple-element.11), channel_id=1, replica_groups={{15,14,13,12,11,10,9,8,7,6,5,4,3,2,1,0},{31,30,29,28,27,26,25,24,23,22,..., dimensions={0} | all-to-all | bytes 655360 | tf_op jit(solution)/shard_map/all_to_all | solution.py:353
  24.1 0.6 shard_map.114
  24.7 0.0 copy-start
  24.7 2.0 %collective-permute-start = (f32[8,40,128]{2,1,0:T(8,128)S(1)}, f32[8,40,128]{2,1,0:T(8,128)S(1)}, u32[]{:S(2)}, u32[]{:S(2)}) collective-permute-start(f32[8,40,128]{2,1,0:T(8,128)S(1)} %get-tuple-element.12), channel_id=1, source_target_pairs={{8,16},{16,8},{9,17},{17,9},{10,18},{18,10},{11,19},{19,11},{12,20... | collective-permute-start | bytes 491528 | tf_op jit(solution)/shard_map/ppermute | solution.py:358
  26.7 0.0 copy-start.1
  26.7 0.0 copy-start.2
  26.8 0.0 copy-start.3
  26.8 13.3 %all-to-all-start.1 = ((f32[32,1,128]{2,1,0:T(1,128)}), f32[32,1,128]{2,1,0:T(1,128)S(1)}, u32[]{:S(2)}, u32[]{:S(2)}) async-start(f32[32,1,128]{2,1,0:T(1,128)} %get-tuple-element.13), calls=%async_computation.1 | async-start | bytes 32768 | tf_op jit(solution)/shard_map/all_to_all | solution.py:359
  40.1 0.0 collective-permute-done.dyn_halo.static_halo
  40.1 0.0 copy-done
  40.1 0.0 copy-done.1
  40.1 0.0 copy-done.2
  40.2 0.0 copy-done.3
  40.2 5.4 %shard_map.115.near = f32[16,128]{1,0:T(8,128)S(1)} custom-call(s32[4,8]{1,0:T(4,128)S(1)} %copy-done.1, s32[4,4]{1,0:T(4,128)S(1)} %copy-done.2, s32[3,8]{1,0:T(4,128)S(1)} %copy-done.3, f32[48,128]{1,0:T(8,128)S(1)} %copy-done, f32[16,40,128]{2,1,0:T(8,128)S(1)} %all_to_all.30.dyn.static, f32[8,40,128]{2,1,0:T(8,128)S(1)} %collective-permute-done.dyn_halo.static_halo, ...), custom_call_target="tpu_custom_call" | custom-call | flops 40000000 | bytes 1000 | tf_op jit(solution)/shard_map/pallas_call | solution.py:34
  45.5 0.0 all-to-all-done.1.far
  45.5 0.4 shard_map.116
  45.9 12.6 %all_to_all.31.dyn = f32[16,16,128]{2,1,0:T(8,128)S(1)} all-to-all(f32[16,16,128]{2,1,0:T(8,128)S(1)} %shard_map.116), channel_id=1, replica_groups={{15,14,13,12,11,10,9,8,7,6,5,4,3,2,1,0},{31,30,29,28,27,26,25,24,23,22,..., dimensions={0} | all-to-all | bytes 262144 | tf_op jit(solution)/shard_map/all_to_all | solution.py:353
  58.5 0.6 shard_map.117
  59.1 3.0 %collective-permute-start.1 = (f32[8,16,128]{2,1,0:T(8,128)S(1)}, f32[8,16,128]{2,1,0:T(8,128)S(1)}, u32[]{:S(2)}, u32[]{:S(2)}) collective-permute-start(f32[8,16,128]{2,1,0:T(8,128)S(1)} %get-tuple-element.14), channel_id=1, source_target_pairs={{8,16},{16,8},{9,17},{17,9},{10,18},{18,10},{11,19},{19,11},{12,20... | collective-permute-start | bytes 196616 | tf_op jit(solution)/shard_map/ppermute | solution.py:358
  62.1 8.4 %all-to-all-start.3 = ((f32[32,1,128]{2,1,0:T(1,128)}), f32[32,1,128]{2,1,0:T(1,128)S(1)}, u32[]{:S(2)}, u32[]{:S(2)}) async-start(f32[32,1,128]{2,1,0:T(1,128)} %get-tuple-element.15), calls=%async_computation.3 | async-start | bytes 32768 | tf_op jit(solution)/shard_map/all_to_all | solution.py:359
  70.5 0.0 collective-permute-done.1.dyn_halo
  70.5 5.4 %shard_map.118.near = f32[16,128]{1,0:T(8,128)S(1)} custom-call(s32[4,8]{1,0:T(4,128)S(1)} %copy-done.1, s32[4,4]{1,0:T(4,128)S(1)} %copy-done.2, s32[3,8]{1,0:T(4,128)S(1)} %copy-done.3, f32[48,128]{1,0:T(8,128)S(1)} %copy-done, f32[16,16,128]{2,1,0:T(8,128)S(1)} %all_to_all.31.dyn, f32[8,16,128]{2,1,0:T(8,128)S(1)} %collective-permute-done.1.dyn_halo, ...), custom_call_target="tpu_custom_call" | custom-call | flops 40000000 | bytes 1000 | tf_op jit(solution)/shard_map/pallas_call | solution.py:34
  75.9 0.0 all-to-all-done.3.far
  75.9 0.4 shard_map.119
  76.2 12.1 %all_to_all.32.dyn = f32[16,16,128]{2,1,0:T(8,128)S(1)} all-to-all(f32[16,16,128]{2,1,0:T(8,128)S(1)} %shard_map.119), channel_id=1, replica_groups={{15,14,13,12,11,10,9,8,7,6,5,4,3,2,1,0},{31,30,29,28,27,26,25,24,23,22,..., dimensions={0} | all-to-all | bytes 262144 | tf_op jit(solution)/shard_map/all_to_all | solution.py:353
  88.3 0.6 shard_map.120
  88.9 3.0 %collective-permute-start.2 = (f32[8,16,128]{2,1,0:T(8,128)S(1)}, f32[8,16,128]{2,1,0:T(8,128)S(1)}, u32[]{:S(2)}, u32[]{:S(2)}) collective-permute-start(f32[8,16,128]{2,1,0:T(8,128)S(1)} %get-tuple-element.16), channel_id=1, source_target_pairs={{8,16},{16,8},{9,17},{17,9},{10,18},{18,10},{11,19},{19,11},{12,20... | collective-permute-start | bytes 196616 | tf_op jit(solution)/shard_map/ppermute | solution.py:358
  91.9 8.3 %all-to-all-start.5 = ((f32[32,1,128]{2,1,0:T(1,128)}), f32[32,1,128]{2,1,0:T(1,128)S(1)}, u32[]{:S(2)}, u32[]{:S(2)}) async-start(f32[32,1,128]{2,1,0:T(1,128)} %get-tuple-element.17), calls=%async_computation.5 | async-start | bytes 32768 | tf_op jit(solution)/shard_map/all_to_all | solution.py:359
  100.3 0.0 collective-permute-done.2.dyn_halo
  100.3 5.4 %shard_map.121.near = f32[16,128]{1,0:T(8,128)S(1)} custom-call(s32[4,8]{1,0:T(4,128)S(1)} %copy-done.1, s32[4,4]{1,0:T(4,128)S(1)} %copy-done.2, s32[3,8]{1,0:T(4,128)S(1)} %copy-done.3, f32[48,128]{1,0:T(8,128)S(1)} %copy-done, f32[16,16,128]{2,1,0:T(8,128)S(1)} %all_to_all.32.dyn, f32[8,16,128]{2,1,0:T(8,128)S(1)} %collective-permute-done.2.dyn_halo, ...), custom_call_target="tpu_custom_call" | custom-call | flops 40000000 | bytes 1000 | tf_op jit(solution)/shard_map/pallas_call | solution.py:34
  105.7 0.0 all-to-all-done.5.far
  105.7 0.8 shard_map.122
Async XLA Ops:
  24.7 15.5 %copy-start = (f32[48,128]{1,0:T(8,128)S(1)}, f32[48,128]{1,0:T(8,128)}, u32[]{:S(2)}) copy-start(f32[48,128]{1,0:T(8,128)} %get-tuple-element.10.own) | copy-start | bytes 73732
  24.7 15.4 %collective-permute-start = (f32[8,40,128]{2,1,0:T(8,128)S(1)}, f32[8,40,128]{2,1,0:T(8,128)S(1)}, u32[]{:S(2)}, u32[]{:S(2)}) collective-permute-start(f32[8,40,128]{2,1,0:T(8,128)S(1)} %get-tuple-element.12), channel_id=1, source_target_pairs={{8,16},{16,8},{9,17},{17,9},{10,18},{18,10},{11,19},{19,11},{12,20... | collective-permute-start | bytes 491528 | tf_op jit(solution)/shard_map/ppermute | solution.py:358
  26.7 13.4 %copy-start.1 = (s32[4,8]{1,0:T(4,128)S(1)}, s32[4,8]{1,0:T(4,128)}, u32[]{:S(2)}) copy-start(s32[4,8]{1,0:T(4,128)} %near.5) | copy-start | bytes 388
  26.7 13.4 %copy-start.2 = (s32[4,4]{1,0:T(4,128)S(1)}, s32[4,4]{1,0:T(4,128)}, u32[]{:S(2)}) copy-start(s32[4,4]{1,0:T(4,128)} %grids.5) | copy-start | bytes 196
  26.8 13.4 %copy-start.3 = (s32[3,8]{1,0:T(4,128)S(1)}, s32[3,8]{1,0:T(4,128)}, u32[]{:S(2)}) copy-start(s32[3,8]{1,0:T(4,128)} %sources.5) | copy-start | bytes 292
  26.8 18.8 %all-to-all-start.1 = ((f32[32,1,128]{2,1,0:T(1,128)}), f32[32,1,128]{2,1,0:T(1,128)S(1)}, u32[]{:S(2)}, u32[]{:S(2)}) async-start(f32[32,1,128]{2,1,0:T(1,128)} %get-tuple-element.13), calls=%async_computation.1 | async-start | bytes 32768 | tf_op jit(solution)/shard_map/all_to_all | solution.py:359
  59.1 11.4 %collective-permute-start.1 = (f32[8,16,128]{2,1,0:T(8,128)S(1)}, f32[8,16,128]{2,1,0:T(8,128)S(1)}, u32[]{:S(2)}, u32[]{:S(2)}) collective-permute-start(f32[8,16,128]{2,1,0:T(8,128)S(1)} %get-tuple-element.14), channel_id=1, source_target_pairs={{8,16},{16,8},{9,17},{17,9},{10,18},{18,10},{11,19},{19,11},{12,20... | collective-permute-start | bytes 196616 | tf_op jit(solution)/shard_map/ppermute | solution.py:358
  62.1 13.7 %all-to-all-start.3 = ((f32[32,1,128]{2,1,0:T(1,128)}), f32[32,1,128]{2,1,0:T(1,128)S(1)}, u32[]{:S(2)}, u32[]{:S(2)}) async-start(f32[32,1,128]{2,1,0:T(1,128)} %get-tuple-element.15), calls=%async_computation.3 | async-start | bytes 32768 | tf_op jit(solution)/shard_map/all_to_all | solution.py:359
  88.9 11.4 %collective-permute-start.2 = (f32[8,16,128]{2,1,0:T(8,128)S(1)}, f32[8,16,128]{2,1,0:T(8,128)S(1)}, u32[]{:S(2)}, u32[]{:S(2)}) collective-permute-start(f32[8,16,128]{2,1,0:T(8,128)S(1)} %get-tuple-element.16), channel_id=1, source_target_pairs={{8,16},{16,8},{9,17},{17,9},{10,18},{18,10},{11,19},{19,11},{12,20... | collective-permute-start | bytes 196616 | tf_op jit(solution)/shard_map/ppermute | solution.py:358
  91.9 13.7 %all-to-all-start.5 = ((f32[32,1,128]{2,1,0:T(1,128)}), f32[32,1,128]{2,1,0:T(1,128)S(1)}, u32[]{:S(2)}, u32[]{:S(2)}) async-start(f32[32,1,128]{2,1,0:T(1,128)} %get-tuple-element.17), calls=%async_computation.5 | async-start | bytes 32768 | tf_op jit(solution)/shard_map/all_to_all | solution.py:359

commit v5 on v4

--- a/solution.py
+++ b/solution.py
@@ -109,14 +109,15 @@
     for k in range(CORES):
         total = None
         for g in range(GROUPS):
-            part = dyn[MEMBERS - 1 - k * GROUPS - g, 15:16, :]
+            part = dyn[place_of(k, g), 15:16, :]
             total = part if total is None else total + part
         totals.append(total)
     lane = lax.broadcasted_iota(jnp.int32, (1, LANES), 1)
     row = jnp.where(lane < 8, totals[0], totals[1])
     for i in range(CHIPS):
         far[i] = row
-    halo[...] = dyn[pl.ds((CORES - 1 - core) * GROUPS, GROUPS)]
+    for g in range(GROUPS):
+        halo[g] = dyn[place_of(core, g)]
 
 
 def geometry(t, s):
@@ -130,15 +131,16 @@
 
 
 def near_kernel(
-    near, grids, sources, own, dyn, dyn_halo, static, static_halo, result, columns, sums, moving, fixed
+    lists, own, dyn, dyn_halo, static, static_halo, result, columns, sums, moving, fixed
 ):
     core, _ = position()
     for m in range(MEMBERS):
-        moving[m] = dyn[MEMBERS - 1 - m, 0:DYN, :]
-        fixed[m] = static[MEMBERS - 1 - m, SITE:FIRST, :]
+        at = place_of(m // GROUPS, m % GROUPS)
+        moving[m] = dyn[at, 0:DYN, :]
+        fixed[m] = static[at, SITE:FIRST, :]
     for g in range(GROUPS):
-        moving[MEMBERS + g] = dyn_halo[GROUPS - 1 - g, 0:DYN, :]
-        fixed[MEMBERS + g] = static_halo[GROUPS - 1 - g, SITE:FIRST, :]
+        moving[MEMBERS + g] = dyn_halo[g, 0:DYN, :]
+        fixed[MEMBERS + g] = static_halo[g, SITE:FIRST, :]
     for r in range(3 * AB + 3 * GB):
         columns[r] = jnp.transpose(jnp.broadcast_to(own[r : r + 1, :], (LANES, LANES)))
 
@@ -178,7 +180,7 @@
             if n == 0:
                 share, b = me, tb
             else:
-                share, b = place(near[tb, n - 1], AB)
+                share, b = place(lists[tb, n - 1], AB)
             s, m, m3 = dipole_terms(share, b)
             dx, dy, dz, cube, square = geometry(t, s)
             weight = (m3[0] * dx + m3[1] * dy + m3[2] * dz) * (cube * square)
@@ -190,7 +192,7 @@
                 weight = jnp.where(other, weight, 0.0)
             acc = [acc[a] + (weight * d - m[a] * cube) for a, d in enumerate((dx, dy, dz))]
         for n in range(4):
-            share, b = place(grids[tb, n], GB)
+            share, b = place(lists[AB + tb, n], GB)
             s = rows(fixed, share, 12 + b, GB)
             q = moving[share, pl.ds(12 + b, 1), :]
             dx, dy, dz, cube, _ = geometry(t, s)
@@ -206,7 +208,7 @@
         t = [columns[12 + a * GB + tb, pl.ds(start, CHUNK), :] for a in range(3)]
         acc = jnp.zeros((CHUNK, LANES), jnp.float32)
         for n in range(8):
-            share, b = place(sources[tb, n], AB)
+            share, b = place(lists[2 * AB + tb, n], AB)
             s = rows(fixed, share, b, AB)
             m = rows(moving, share, b, AB)
             dx, dy, dz, cube, _ = geometry(t, s)
@@ -304,7 +306,12 @@
 
 
 def columns():
-    return [[chip * MEMBERS + m for m in reversed(range(MEMBERS))] for chip in range(CHIPS)]
+    order = [k * GROUPS + g for g in reversed(range(GROUPS)) for k in reversed(range(CORES))]
+    return [[chip * MEMBERS + m for m in order] for chip in range(CHIPS)]
+
+
+def place_of(core, group):
+    return (GROUPS - 1 - group) * CORES + (CORES - 1 - core)
 
 
 def planes():
@@ -346,6 +353,7 @@
         pltpu.VMEM((7 * VECTORS, 8, LANES), jnp.float32),
     ]
     static = static_halo = None
+    lists = jnp.concatenate([near, jnp.pad(grids, ((0, 0), (0, 4))), sources])
     every = ("x", "z", "core", "grp")
     for iteration in range(ITERS):
         last = iteration == ITERS - 1
@@ -361,8 +369,8 @@
         near_field = call(
             near_kernel,
             out(16, LANES),
-            (near, grids, sources, own, dyn, halo, static, static_halo),
-            specs=[SM] * 3 + [VM] * 5,
+            (lists, own, dyn, halo, static, static_halo),
+            specs=[SM] + [VM] * 5,
             flops=40_000_000,
             scratch=[
                 pltpu.VMEM((21, LANES, LANES), jnp.float32),

time: 107 us -> 107 us (level)
    ppermute x3, starting transfers between devices: 8.06 us -> 6.73 us  [body(): halo = lax.ppermute(halo_out, every, swaps())]
where the time goes in v5:
time: 107 us; the launch traced here: 106 us
  blocking collectives  46.3 us (43%)
  starting transfers between devices  37.5 us (35%)
  Pallas kernels  21.4 us (20%)
    all_to_all x3, blocking collectives, body(): lax.all_to_all(copies, every, 0, 0, axis_index_groups=columns(), tiled=True)  46.3 us
    all_to_all x3, starting transfers between devices, body(): lax.all_to_all(far_out, every, 0, 0, axis_index_groups=planes(), tiled=True)  30.8 us
    pallas_call x10, Pallas kernels, call(): pl.pallas_call(kernel, out_shape=outs, in_specs=specs or [VM] * len(args)...  21.4 us
    ppermute x3, starting transfers between devices, body(): halo = lax.ppermute(halo_out, every, swaps())  6.73 us
  transfers between devices with their start and end apart: 6, of which 0 were waited for; matrix products, arithmetic and copies ran while one was open for 0% of the time, Pallas kernels for 15%

profile of v5, /device:TPU:1, one launch (start us, length us, event | category | flops | bytes accessed | tf_op | source)
XLA Modules:
  0.0 106.0 jit_solution(11563367856237064605)
XLA Ops:
  0.6 1.8 %shard_map.113 = (f32[48,128]{1,0:T(8,128)}, f32[16,40,128]{2,1,0:T(8,128)}) custom-call(f32[3,512]{1,0:T(4,128)} %sites.1, f32[3,384]{1,0:T(4,128)} %points.1, f32[3,512]{1,0:T(4,128)} %guess.1, f32[3,512]{1,0:T(4,128)} %fixed.1, f32[512]{0:T(512)} %pol.1, f32[384]{0:T(512)} %base.1, f32[384]{0:T(512)} %resp.1), custom_call_target="tpu_custom_call" | custom-call | flops 1000000 | bytes 1000 | tf_op jit(solution)/shard_map/pallas_call | solution.py:34
  2.4 20.2 %all_to_all.30.dyn.static = f32[16,40,128]{2,1,0:T(8,128)S(1)} all-to-all(f32[16,40,128]{2,1,0:T(8,128)} %get-tuple-element.11), channel_id=1, replica_groups={{15,7,14,6,13,5,12,4,11,3,10,2,9,1,8,0},{31,23,30,22,29,21,28,20,27,19,..., dimensions={0} | all-to-all | bytes 655360 | tf_op jit(solution)/shard_map/all_to_all | solution.py:361
  22.7 0.6 shard_map.114
  23.3 1.9 %collective-permute-start = (f32[8,40,128]{2,1,0:T(8,128)S(1)}, f32[8,40,128]{2,1,0:T(8,128)S(1)}, u32[]{:S(2)}, u32[]{:S(2)}) collective-permute-start(f32[8,40,128]{2,1,0:T(8,128)S(1)} %get-tuple-element.12), channel_id=1, source_target_pairs={{8,16},{16,8},{9,17},{17,9},{10,18},{18,10},{11,19},{19,11},{12,20... | collective-permute-start | bytes 491528 | tf_op jit(solution)/shard_map/ppermute | solution.py:366
  25.2 0.0 copy-start.1
  25.2 0.0 copy-start.2
  25.2 0.0 copy-start.3
  25.2 0.0 copy-start
  25.2 13.8 %all-to-all-start.1 = ((f32[32,1,128]{2,1,0:T(1,128)}), f32[32,1,128]{2,1,0:T(1,128)S(1)}, u32[]{:S(2)}, u32[]{:S(2)}) async-start(f32[32,1,128]{2,1,0:T(1,128)} %get-tuple-element.13), calls=%async_computation.1 | async-start | bytes 32768 | tf_op jit(solution)/shard_map/all_to_all | solution.py:367
  39.0 0.0 copy-done.1
  39.1 0.0 copy-done.2
  39.1 0.0 copy-done.3
  39.1 0.0 collective-permute-done.dyn_halo.static_halo
  39.1 0.0 copy-done
  39.1 5.4 %shard_map.115.near = f32[16,128]{1,0:T(8,128)S(1)} custom-call(s32[11,8]{1,0:T(8,128)S(1)} %fusion.lists, f32[48,128]{1,0:T(8,128)S(1)} %copy-done, f32[16,40,128]{2,1,0:T(8,128)S(1)} %all_to_all.30.dyn.static, f32[8,40,128]{2,1,0:T(8,128)S(1)} %collective-permute-done.dyn_halo.static_halo, f32[16,40,128]{2,1,0:T(8,128)S(1)} %all_to_all.30.dyn.static, ...), custom_call_target="tpu_custom_call" | custom-call | flops 40000000 | bytes 1000 | tf_op jit(solution)/shard_map/pallas_call | solution.py:34
  44.5 0.0 all-to-all-done.1.far
  44.5 0.4 shard_map.116
  44.9 13.4 %all_to_all.31.dyn = f32[16,16,128]{2,1,0:T(8,128)S(1)} all-to-all(f32[16,16,128]{2,1,0:T(8,128)S(1)} %shard_map.116), channel_id=1, replica_groups={{15,7,14,6,13,5,12,4,11,3,10,2,9,1,8,0},{31,23,30,22,29,21,28,20,27,19,..., dimensions={0} | all-to-all | bytes 262144 | tf_op jit(solution)/shard_map/all_to_all | solution.py:361
  58.3 0.6 shard_map.117
  58.9 2.4 %collective-permute-start.1 = (f32[8,16,128]{2,1,0:T(8,128)S(1)}, f32[8,16,128]{2,1,0:T(8,128)S(1)}, u32[]{:S(2)}, u32[]{:S(2)}) collective-permute-start(f32[8,16,128]{2,1,0:T(8,128)S(1)} %get-tuple-element.14), channel_id=1, source_target_pairs={{8,16},{16,8},{9,17},{17,9},{10,18},{18,10},{11,19},{19,11},{12,20... | collective-permute-start | bytes 196616 | tf_op jit(solution)/shard_map/ppermute | solution.py:366
  61.4 8.5 %all-to-all-start.3 = ((f32[32,1,128]{2,1,0:T(1,128)}), f32[32,1,128]{2,1,0:T(1,128)S(1)}, u32[]{:S(2)}, u32[]{:S(2)}) async-start(f32[32,1,128]{2,1,0:T(1,128)} %get-tuple-element.15), calls=%async_computation.3 | async-start | bytes 32768 | tf_op jit(solution)/shard_map/all_to_all | solution.py:367
  69.8 0.0 collective-permute-done.1.dyn_halo
  69.8 5.4 %shard_map.118.near = f32[16,128]{1,0:T(8,128)S(1)} custom-call(s32[11,8]{1,0:T(8,128)S(1)} %fusion.lists, f32[48,128]{1,0:T(8,128)S(1)} %copy-done, f32[16,16,128]{2,1,0:T(8,128)S(1)} %all_to_all.31.dyn, f32[8,16,128]{2,1,0:T(8,128)S(1)} %collective-permute-done.1.dyn_halo, f32[16,40,128]{2,1,0:T(8,128)S(1)} %all_to_all.30.dyn.static, ...), custom_call_target="tpu_custom_call" | custom-call | flops 40000000 | bytes 1000 | tf_op jit(solution)/shard_map/pallas_call | solution.py:34
  75.2 0.0 all-to-all-done.3.far
  75.3 0.4 shard_map.119
  75.6 12.7 %all_to_all.32.dyn = f32[16,16,128]{2,1,0:T(8,128)S(1)} all-to-all(f32[16,16,128]{2,1,0:T(8,128)S(1)} %shard_map.119), channel_id=1, replica_groups={{15,7,14,6,13,5,12,4,11,3,10,2,9,1,8,0},{31,23,30,22,29,21,28,20,27,19,..., dimensions={0} | all-to-all | bytes 262144 | tf_op jit(solution)/shard_map/all_to_all | solution.py:361
  88.3 0.6 shard_map.120
  88.9 2.4 %collective-permute-start.2 = (f32[8,16,128]{2,1,0:T(8,128)S(1)}, f32[8,16,128]{2,1,0:T(8,128)S(1)}, u32[]{:S(2)}, u32[]{:S(2)}) collective-permute-start(f32[8,16,128]{2,1,0:T(8,128)S(1)} %get-tuple-element.16), channel_id=1, source_target_pairs={{8,16},{16,8},{9,17},{17,9},{10,18},{18,10},{11,19},{19,11},{12,20... | collective-permute-start | bytes 196616 | tf_op jit(solution)/shard_map/ppermute | solution.py:366
  91.3 8.5 %all-to-all-start.5 = ((f32[32,1,128]{2,1,0:T(1,128)}), f32[32,1,128]{2,1,0:T(1,128)S(1)}, u32[]{:S(2)}, u32[]{:S(2)}) async-start(f32[32,1,128]{2,1,0:T(1,128)} %get-tuple-element.17), calls=%async_computation.5 | async-start | bytes 32768 | tf_op jit(solution)/shard_map/all_to_all | solution.py:367
  99.8 0.0 collective-permute-done.2.dyn_halo
  99.8 5.4 %shard_map.121.near = f32[16,128]{1,0:T(8,128)S(1)} custom-call(s32[11,8]{1,0:T(8,128)S(1)} %fusion.lists, f32[48,128]{1,0:T(8,128)S(1)} %copy-done, f32[16,16,128]{2,1,0:T(8,128)S(1)} %all_to_all.32.dyn, f32[8,16,128]{2,1,0:T(8,128)S(1)} %collective-permute-done.2.dyn_halo, f32[16,40,128]{2,1,0:T(8,128)S(1)} %all_to_all.30.dyn.static, ...), custom_call_target="tpu_custom_call" | custom-call | flops 40000000 | bytes 1000 | tf_op jit(solution)/shard_map/pallas_call | solution.py:34
  105.2 0.0 all-to-all-done.5.far
  105.2 0.8 shard_map.122
  (1 shorter events, 0.0 us)
Async XLA Ops:
  23.3 15.8 %collective-permute-start = (f32[8,40,128]{2,1,0:T(8,128)S(1)}, f32[8,40,128]{2,1,0:T(8,128)S(1)}, u32[]{:S(2)}, u32[]{:S(2)}) collective-permute-start(f32[8,40,128]{2,1,0:T(8,128)S(1)} %get-tuple-element.12), channel_id=1, source_target_pairs={{8,16},{16,8},{9,17},{17,9},{10,18},{18,10},{11,19},{19,11},{12,20... | collective-permute-start | bytes 491528 | tf_op jit(solution)/shard_map/ppermute | solution.py:366
  25.2 13.9 %copy-start.1 = (s32[4,4]{1,0:T(4,128)S(1)}, s32[4,4]{1,0:T(4,128)}, u32[]{:S(2)}) copy-start(s32[4,4]{1,0:T(4,128)} %param.18) | copy-start | bytes 196
  25.2 13.9 %copy-start.2 = (s32[3,8]{1,0:T(4,128)S(1)}, s32[3,8]{1,0:T(4,128)}, u32[]{:S(2)}) copy-start(s32[3,8]{1,0:T(4,128)} %param.19) | copy-start | bytes 292
  25.2 13.9 %copy-start.3 = (s32[4,8]{1,0:T(4,128)S(1)}, s32[4,8]{1,0:T(4,128)}, u32[]{:S(2)}) copy-start(s32[4,8]{1,0:T(4,128)} %param.17) | copy-start | bytes 388
  25.2 13.9 %copy-start = (f32[48,128]{1,0:T(8,128)S(1)}, f32[48,128]{1,0:T(8,128)}, u32[]{:S(2)}) copy-start(f32[48,128]{1,0:T(8,128)} %get-tuple-element.10.own) | copy-start | bytes 73732
  25.2 19.3 %all-to-all-start.1 = ((f32[32,1,128]{2,1,0:T(1,128)}), f32[32,1,128]{2,1,0:T(1,128)S(1)}, u32[]{:S(2)}, u32[]{:S(2)}) async-start(f32[32,1,128]{2,1,0:T(1,128)} %get-tuple-element.13), calls=%async_computation.1 | async-start | bytes 32768 | tf_op jit(solution)/shard_map/all_to_all | solution.py:367
  58.9 10.9 %collective-permute-start.1 = (f32[8,16,128]{2,1,0:T(8,128)S(1)}, f32[8,16,128]{2,1,0:T(8,128)S(1)}, u32[]{:S(2)}, u32[]{:S(2)}) collective-permute-start(f32[8,16,128]{2,1,0:T(8,128)S(1)} %get-tuple-element.14), channel_id=1, source_target_pairs={{8,16},{16,8},{9,17},{17,9},{10,18},{18,10},{11,19},{19,11},{12,20... | collective-permute-start | bytes 196616 | tf_op jit(solution)/shard_map/ppermute | solution.py:366
  61.4 13.9 %all-to-all-start.3 = ((f32[32,1,128]{2,1,0:T(1,128)}), f32[32,1,128]{2,1,0:T(1,128)S(1)}, u32[]{:S(2)}, u32[]{:S(2)}) async-start(f32[32,1,128]{2,1,0:T(1,128)} %get-tuple-element.15), calls=%async_computation.3 | async-start | bytes 32768 | tf_op jit(solution)/shard_map/all_to_all | solution.py:367
  88.9 10.9 %collective-permute-start.2 = (f32[8,16,128]{2,1,0:T(8,128)S(1)}, f32[8,16,128]{2,1,0:T(8,128)S(1)}, u32[]{:S(2)}, u32[]{:S(2)}) collective-permute-start(f32[8,16,128]{2,1,0:T(8,128)S(1)} %get-tuple-element.16), channel_id=1, source_target_pairs={{8,16},{16,8},{9,17},{17,9},{10,18},{18,10},{11,19},{19,11},{12,20... | collective-permute-start | bytes 196616 | tf_op jit(solution)/shard_map/ppermute | solution.py:366
  91.3 13.9 %all-to-all-start.5 = ((f32[32,1,128]{2,1,0:T(1,128)}), f32[32,1,128]{2,1,0:T(1,128)S(1)}, u32[]{:S(2)}, u32[]{:S(2)}) async-start(f32[32,1,128]{2,1,0:T(1,128)} %get-tuple-element.17), calls=%async_computation.5 | async-start | bytes 32768 | tf_op jit(solution)/shard_map/all_to_all | solution.py:367

commit v6 on v5

--- a/solution.py
+++ b/solution.py
@@ -131,8 +131,10 @@
 
 
 def near_kernel(
-    lists, own, dyn, dyn_halo, static, static_halo, result, columns, sums, moving, fixed
+    given, own, dyn, dyn_halo, static, static_halo, result, columns, sums, moving, fixed, lists, sem
 ):
+    move = pltpu.make_async_copy(given, lists, sem)
+    move.start()
     core, _ = position()
     for m in range(MEMBERS):
         at = place_of(m // GROUPS, m % GROUPS)
@@ -167,6 +169,7 @@
         return s, m, [3.0 * v for v in m]
 
     me = second + lax.axis_index("grp")
+    move.wait()
 
     def finished(r):
         result[r : r + 1, :] = jnp.sum(jnp.transpose(sums[r]), axis=0, keepdims=True)
@@ -370,13 +373,15 @@
             near_kernel,
             out(16, LANES),
             (lists, own, dyn, halo, static, static_halo),
-            specs=[SM] + [VM] * 5,
+            specs=[ANY] + [VM] * 5,
             flops=40_000_000,
             scratch=[
                 pltpu.VMEM((21, LANES, LANES), jnp.float32),
                 pltpu.VMEM((15, LANES, LANES), jnp.float32),
                 pltpu.VMEM((MEMBERS + GROUPS, DYN, LANES), jnp.float32),
                 pltpu.VMEM((MEMBERS + GROUPS, FIRST - SITE, LANES), jnp.float32),
+                pltpu.SMEM(lists.shape, jnp.int32),
+                pltpu.SemaphoreType.DMA(()),
             ],
             limit=16 << 20,
         )

time: 107 us -> 107 us (level)
  Pallas kernels: 21.4 us -> 20.3 us
  transfers between devices with their start and end apart: 6 -> 6, of which waited for: 0 -> 0; matrix products, arithmetic and copies ran while one was open for 0% -> 0% of each run, Pallas kernels for 15% -> 14%
where the time goes in v6:
time: 107 us; the launch traced here: 105 us
  blocking collectives  47.3 us (44%)
  starting transfers between devices  36.8 us (34%)
  Pallas kernels  20.3 us (19%)
    all_to_all x3, blocking collectives, body(): lax.all_to_all(copies, every, 0, 0, axis_index_groups=columns(), tiled=True)  47.3 us
    all_to_all x3, starting transfers between devices, body(): lax.all_to_all(far_out, every, 0, 0, axis_index_groups=planes(), tiled=True)  30.7 us
    pallas_call x10, Pallas kernels, call(): pl.pallas_call(kernel, out_shape=outs, in_specs=specs or [VM] * len(args)...  20.3 us
    ppermute x3, starting transfers between devices, body(): halo = lax.ppermute(halo_out, every, swaps())  6.06 us
  transfers between devices with their start and end apart: 6, of which 0 were waited for; matrix products, arithmetic and copies ran while one was open for 0% of the time, Pallas kernels for 14%

profile of v6, /device:TPU:1, one launch (start us, length us, event | category | flops | bytes accessed | tf_op | source)
XLA Modules:
  0.0 105.3 jit_solution(6074570106551184148)
XLA Ops:
  0.6 1.8 %shard_map.113 = (f32[48,128]{1,0:T(8,128)}, f32[16,40,128]{2,1,0:T(8,128)}) custom-call(f32[3,512]{1,0:T(4,128)} %sites.1, f32[3,384]{1,0:T(4,128)} %points.1, f32[3,512]{1,0:T(4,128)} %guess.1, f32[3,512]{1,0:T(4,128)} %fixed.1, f32[512]{0:T(512)} %pol.1, f32[384]{0:T(512)} %base.1, f32[384]{0:T(512)} %resp.1), custom_call_target="tpu_custom_call" | custom-call | flops 1000000 | bytes 1000 | tf_op jit(solution)/shard_map/pallas_call | solution.py:34
  2.4 20.2 %all_to_all.30.dyn.static = f32[16,40,128]{2,1,0:T(8,128)S(1)} all-to-all(f32[16,40,128]{2,1,0:T(8,128)} %get-tuple-element.11), channel_id=1, replica_groups={{15,7,14,6,13,5,12,4,11,3,10,2,9,1,8,0},{31,23,30,22,29,21,28,20,27,19,..., dimensions={0} | all-to-all | bytes 655360 | tf_op jit(solution)/shard_map/all_to_all | solution.py:364
  22.7 0.6 shard_map.114
  23.3 1.9 %collective-permute-start = (f32[8,40,128]{2,1,0:T(8,128)S(1)}, f32[8,40,128]{2,1,0:T(8,128)S(1)}, u32[]{:S(2)}, u32[]{:S(2)}) collective-permute-start(f32[8,40,128]{2,1,0:T(8,128)S(1)} %get-tuple-element.12), channel_id=1, source_target_pairs={{8,16},{16,8},{9,17},{17,9},{10,18},{18,10},{11,19},{19,11},{12,20... | collective-permute-start | bytes 491528 | tf_op jit(solution)/shard_map/ppermute | solution.py:369
  25.2 0.0 copy-start.1
  25.2 0.0 copy-start.2
  25.2 0.0 copy-start.3
  25.2 0.0 copy-start
  25.2 13.8 %all-to-all-start.1 = ((f32[32,1,128]{2,1,0:T(1,128)}), f32[32,1,128]{2,1,0:T(1,128)S(1)}, u32[]{:S(2)}, u32[]{:S(2)}) async-start(f32[32,1,128]{2,1,0:T(1,128)} %get-tuple-element.13), calls=%async_computation.1 | async-start | bytes 32768 | tf_op jit(solution)/shard_map/all_to_all | solution.py:370
  39.0 0.0 copy-done.1
  39.1 0.0 copy-done.2
  39.1 0.0 copy-done.3
  39.1 0.0 collective-permute-done.dyn_halo.static_halo
  39.1 0.0 copy-done
  39.1 5.0 %shard_map.115.near = f32[16,128]{1,0:T(8,128)S(1)} custom-call(s32[11,8]{1,0:T(8,128)S(1)} %fusion.given, f32[48,128]{1,0:T(8,128)S(1)} %copy-done, f32[16,40,128]{2,1,0:T(8,128)S(1)} %all_to_all.30.dyn.static, f32[8,40,128]{2,1,0:T(8,128)S(1)} %collective-permute-done.dyn_halo.static_halo, f32[16,40,128]{2,1,0:T(8,128)S(1)} %all_to_all.30.dyn.static, ...), custom_call_target="tpu_custom_call" | custom-call | flops 40000000 | bytes 1000 | tf_op jit(solution)/shard_map/pallas_call | solution.py:34
  44.2 0.0 all-to-all-done.1.far
  44.2 0.4 shard_map.116
  44.5 13.8 %all_to_all.31.dyn = f32[16,16,128]{2,1,0:T(8,128)S(1)} all-to-all(f32[16,16,128]{2,1,0:T(8,128)S(1)} %shard_map.116), channel_id=1, replica_groups={{15,7,14,6,13,5,12,4,11,3,10,2,9,1,8,0},{31,23,30,22,29,21,28,20,27,19,..., dimensions={0} | all-to-all | bytes 262144 | tf_op jit(solution)/shard_map/all_to_all | solution.py:364
  58.3 0.6 shard_map.117
  58.9 2.1 %collective-permute-start.1 = (f32[8,16,128]{2,1,0:T(8,128)S(1)}, f32[8,16,128]{2,1,0:T(8,128)S(1)}, u32[]{:S(2)}, u32[]{:S(2)}) collective-permute-start(f32[8,16,128]{2,1,0:T(8,128)S(1)} %get-tuple-element.14), channel_id=1, source_target_pairs={{8,16},{16,8},{9,17},{17,9},{10,18},{18,10},{11,19},{19,11},{12,20... | collective-permute-start | bytes 196616 | tf_op jit(solution)/shard_map/ppermute | solution.py:369
  61.0 8.5 %all-to-all-start.3 = ((f32[32,1,128]{2,1,0:T(1,128)}), f32[32,1,128]{2,1,0:T(1,128)S(1)}, u32[]{:S(2)}, u32[]{:S(2)}) async-start(f32[32,1,128]{2,1,0:T(1,128)} %get-tuple-element.15), calls=%async_computation.3 | async-start | bytes 32768 | tf_op jit(solution)/shard_map/all_to_all | solution.py:370
  69.5 0.0 collective-permute-done.1.dyn_halo
  69.5 5.0 %shard_map.118.near = f32[16,128]{1,0:T(8,128)S(1)} custom-call(s32[11,8]{1,0:T(8,128)S(1)} %fusion.given, f32[48,128]{1,0:T(8,128)S(1)} %copy-done, f32[16,16,128]{2,1,0:T(8,128)S(1)} %all_to_all.31.dyn, f32[8,16,128]{2,1,0:T(8,128)S(1)} %collective-permute-done.1.dyn_halo, f32[16,40,128]{2,1,0:T(8,128)S(1)} %all_to_all.30.dyn.static, ...), custom_call_target="tpu_custom_call" | custom-call | flops 40000000 | bytes 1000 | tf_op jit(solution)/shard_map/pallas_call | solution.py:34
  74.6 0.0 all-to-all-done.3.far
  74.6 0.4 shard_map.119
  74.9 13.3 %all_to_all.32.dyn = f32[16,16,128]{2,1,0:T(8,128)S(1)} all-to-all(f32[16,16,128]{2,1,0:T(8,128)S(1)} %shard_map.119), channel_id=1, replica_groups={{15,7,14,6,13,5,12,4,11,3,10,2,9,1,8,0},{31,23,30,22,29,21,28,20,27,19,..., dimensions={0} | all-to-all | bytes 262144 | tf_op jit(solution)/shard_map/all_to_all | solution.py:364
  88.3 0.6 shard_map.120
  88.9 2.0 %collective-permute-start.2 = (f32[8,16,128]{2,1,0:T(8,128)S(1)}, f32[8,16,128]{2,1,0:T(8,128)S(1)}, u32[]{:S(2)}, u32[]{:S(2)}) collective-permute-start(f32[8,16,128]{2,1,0:T(8,128)S(1)} %get-tuple-element.16), channel_id=1, source_target_pairs={{8,16},{16,8},{9,17},{17,9},{10,18},{18,10},{11,19},{19,11},{12,20... | collective-permute-start | bytes 196616 | tf_op jit(solution)/shard_map/ppermute | solution.py:369
  90.9 8.5 %all-to-all-start.5 = ((f32[32,1,128]{2,1,0:T(1,128)}), f32[32,1,128]{2,1,0:T(1,128)S(1)}, u32[]{:S(2)}, u32[]{:S(2)}) async-start(f32[32,1,128]{2,1,0:T(1,128)} %get-tuple-element.17), calls=%async_computation.5 | async-start | bytes 32768 | tf_op jit(solution)/shard_map/all_to_all | solution.py:370
  99.4 0.0 collective-permute-done.2.dyn_halo
  99.4 5.0 %shard_map.121.near = f32[16,128]{1,0:T(8,128)S(1)} custom-call(s32[11,8]{1,0:T(8,128)S(1)} %fusion.given, f32[48,128]{1,0:T(8,128)S(1)} %copy-done, f32[16,16,128]{2,1,0:T(8,128)S(1)} %all_to_all.32.dyn, f32[8,16,128]{2,1,0:T(8,128)S(1)} %collective-permute-done.2.dyn_halo, f32[16,40,128]{2,1,0:T(8,128)S(1)} %all_to_all.30.dyn.static, ...), custom_call_target="tpu_custom_call" | custom-call | flops 40000000 | bytes 1000 | tf_op jit(solution)/shard_map/pallas_call | solution.py:34
  104.5 0.0 all-to-all-done.5.far
  104.5 0.8 shard_map.122
  (1 shorter events, 0.0 us)
Async XLA Ops:
  23.3 15.8 %collective-permute-start = (f32[8,40,128]{2,1,0:T(8,128)S(1)}, f32[8,40,128]{2,1,0:T(8,128)S(1)}, u32[]{:S(2)}, u32[]{:S(2)}) collective-permute-start(f32[8,40,128]{2,1,0:T(8,128)S(1)} %get-tuple-element.12), channel_id=1, source_target_pairs={{8,16},{16,8},{9,17},{17,9},{10,18},{18,10},{11,19},{19,11},{12,20... | collective-permute-start | bytes 491528 | tf_op jit(solution)/shard_map/ppermute | solution.py:369
  25.2 13.9 %copy-start.1 = (s32[4,4]{1,0:T(4,128)S(1)}, s32[4,4]{1,0:T(4,128)}, u32[]{:S(2)}) copy-start(s32[4,4]{1,0:T(4,128)} %param.18) | copy-start | bytes 196
  25.2 13.9 %copy-start.2 = (s32[3,8]{1,0:T(4,128)S(1)}, s32[3,8]{1,0:T(4,128)}, u32[]{:S(2)}) copy-start(s32[3,8]{1,0:T(4,128)} %param.19) | copy-start | bytes 292
  25.2 13.9 %copy-start.3 = (s32[4,8]{1,0:T(4,128)S(1)}, s32[4,8]{1,0:T(4,128)}, u32[]{:S(2)}) copy-start(s32[4,8]{1,0:T(4,128)} %param.17) | copy-start | bytes 388
  25.2 13.9 %copy-start = (f32[48,128]{1,0:T(8,128)S(1)}, f32[48,128]{1,0:T(8,128)}, u32[]{:S(2)}) copy-start(f32[48,128]{1,0:T(8,128)} %get-tuple-element.10.own) | copy-start | bytes 73732
  25.2 18.9 %all-to-all-start.1 = ((f32[32,1,128]{2,1,0:T(1,128)}), f32[32,1,128]{2,1,0:T(1,128)S(1)}, u32[]{:S(2)}, u32[]{:S(2)}) async-start(f32[32,1,128]{2,1,0:T(1,128)} %get-tuple-element.13), calls=%async_computation.1 | async-start | bytes 32768 | tf_op jit(solution)/shard_map/all_to_all | solution.py:370
  58.9 10.6 %collective-permute-start.1 = (f32[8,16,128]{2,1,0:T(8,128)S(1)}, f32[8,16,128]{2,1,0:T(8,128)S(1)}, u32[]{:S(2)}, u32[]{:S(2)}) collective-permute-start(f32[8,16,128]{2,1,0:T(8,128)S(1)} %get-tuple-element.14), channel_id=1, source_target_pairs={{8,16},{16,8},{9,17},{17,9},{10,18},{18,10},{11,19},{19,11},{12,20... | collective-permute-start | bytes 196616 | tf_op jit(solution)/shard_map/ppermute | solution.py:369
  61.0 13.5 %all-to-all-start.3 = ((f32[32,1,128]{2,1,0:T(1,128)}), f32[32,1,128]{2,1,0:T(1,128)S(1)}, u32[]{:S(2)}, u32[]{:S(2)}) async-start(f32[32,1,128]{2,1,0:T(1,128)} %get-tuple-element.15), calls=%async_computation.3 | async-start | bytes 32768 | tf_op jit(solution)/shard_map/all_to_all | solution.py:370
  88.9 10.5 %collective-permute-start.2 = (f32[8,16,128]{2,1,0:T(8,128)S(1)}, f32[8,16,128]{2,1,0:T(8,128)S(1)}, u32[]{:S(2)}, u32[]{:S(2)}) collective-permute-start(f32[8,16,128]{2,1,0:T(8,128)S(1)} %get-tuple-element.16), channel_id=1, source_target_pairs={{8,16},{16,8},{9,17},{17,9},{10,18},{18,10},{11,19},{19,11},{12,20... | collective-permute-start | bytes 196616 | tf_op jit(solution)/shard_map/ppermute | solution.py:369
  90.9 13.6 %all-to-all-start.5 = ((f32[32,1,128]{2,1,0:T(1,128)}), f32[32,1,128]{2,1,0:T(1,128)S(1)}, u32[]{:S(2)}, u32[]{:S(2)}) async-start(f32[32,1,128]{2,1,0:T(1,128)} %get-tuple-element.17), calls=%async_computation.5 | async-start | bytes 32768 | tf_op jit(solution)/shard_map/all_to_all | solution.py:370
